TPU v7x, 512 devices: a whole 4x8x8 slice. The times are simulated.
512 devices in a mesh: dp: 128 (over x_lo, z, y), mp: 4 (over x_hi, core).
Axes of the slice: x: 4 (x_hi: 2, x_lo: 2; x = x_hi * 2 + x_lo), y: 8, z: 8, core: 2. Of those that a mesh axis runs over, the one named last changes fastest.
Arguments:
- hidden_input: bfloat16 [131072, 384], P('dp'), may hold values from -24 to 24
- output_cotangent: bfloat16 [131072, 8192], P('dp', 'mp'), may hold values from -0.023925781 to 0.023925781
- master_weights: float32 [384, 8192], P('dp', 'mp'), may hold values from -6 to 6
- first_codes: int32 [384, 8192], P('dp', 'mp'), may hold values from 0 to 15
- second_codes: int32 [384, 8192], P('dp', 'mp'), may hold values from 0 to 15
- first_rows: float32 [384], P('dp'), may hold values from 0.001 to 0.03
- first_cols: float32 [8192], P('mp'), may hold values from 0.001 to 0.03
- second_rows: float32 [384], P('dp'), may hold values from 1e-05 to 0.001
- second_cols: float32 [8192], P('mp'), may hold values from 1e-05 to 0.001
- step_count: int32 [], replicated, may hold values from 1 to 9
Outputs:
- new_master: float32 [384, 8192], P('dp', 'mp')
- update_ratio: float32 [384, 8192], P('dp', 'mp')
- gathered_params: bfloat16 [384, 8192], P(None, 'mp')
- first_scaled: float32 [384, 8192], P('dp', 'mp')
- second_scaled: float32 [384, 8192], P('dp', 'mp')
- new_first_rows: float32 [384], P('dp')
- new_first_cols: float32 [8192], P('mp')
- new_second_rows: float32 [384], P('dp')
- new_second_cols: float32 [8192], P('mp')
All inputs are finite; a program needn't handle non-finite values.
Results may differ from a plain program's by a relative error of at most 0.001.
Values may be sent and summed in bfloat16 or wider, within the bound.
A program may use at most 64 MiB of HBM per device.

v0:
```python
import functools

import jax
import jax.numpy as jnp
from jax import lax
from jax.sharding import Mesh
from jax.sharding import PartitionSpec as P

DP = ("dp_0", "dp_1", "dp_2")
DP_MP = ("dp_0", "dp_1", "dp_2", "mp_0", "mp_1")
MP = ("mp_0", "mp_1")


def in_blocks(x, dim, count):
    before, after = (x.shape[:dim], x.shape[dim + 1 :])
    return jnp.moveaxis(x.reshape(*before, count, -1, *after), dim, 0)


def sum_at_owner(x, axis, dim):
    tiles = in_blocks(x, dim, lax.axis_size(axis))
    arrived = lax.all_to_all(tiles, axis, split_axis=0, concat_axis=0, tiled=True)
    return arrived.sum(axis=0)


def sum_by_axis(x, axes, dim):
    far, near = axes
    initial = sum_at_owner(x, far, dim)
    return sum_at_owner(initial, near, dim)


def one_axis_at_a_time(x, axes):
    return functools.reduce(lax.psum, axes, x)


def sent_to_all(x, axis):
    copies = jnp.broadcast_to(x, (lax.axis_size(axis), *x.shape))
    return lax.all_to_all(copies, axis, split_axis=0, concat_axis=0, tiled=True)


def in_order(tiles, dim):
    tiles = jnp.moveaxis(tiles, 0, dim)
    lengths = tiles.shape
    return tiles.reshape(*lengths[:dim], lengths[dim] * lengths[dim + 1], *lengths[dim + 2 :])


def whole_of(x, axes, dim):
    far, near = axes
    tiles = sent_to_all(sent_to_all(x, near), far)
    return in_order(tiles.reshape(-1, *x.shape), dim)


def taken_together(x, axis):
    return sent_to_all(x, axis).max(axis=0)


def in_one(arrays, axis):
    vector, at, outs = (jnp.concatenate([a.reshape(-1) for a in arrays]), 0, [])
    so_far = taken_together(vector, axis)
    for a in arrays:
        outs.append(so_far[at : at + a.size].reshape(a.shape))
        at += a.size
    return tuple(outs)


def by_axis(x, axes):
    far, near = axes
    return taken_together(taken_together(x, near), far)


def together(arrays, axis):
    vector, at, outs = (jnp.concatenate([a.reshape(-1) for a in arrays]), 0, [])
    so_far = by_axis(vector, axis)
    for a in arrays:
        outs.append(so_far[at : at + a.size].reshape(a.shape))
        at += a.size
    return tuple(outs)


def shards(
    hidden_input,
    output_cotangent,
    master_weights,
    first_codes,
    second_codes,
    first_rows,
    first_cols,
    second_rows,
    second_cols,
    step_count,
):
    local_rows = master_weights.shape[0]
    local_cols = master_weights.shape[1]
    gradient = sum_by_axis(
        jnp.dot(hidden_input.T, output_cotangent, preferred_element_type=jnp.float32),
        ("dp_0", ("dp_1", "dp_2")),
        0,
    )
    squares = one_axis_at_a_time(jnp.sum(gradient * gradient), DP_MP)
    entries = local_rows * local_cols * lax.axis_size(DP) * lax.axis_size(MP)
    clipf = jnp.minimum(1.0, 0.01 * jnp.sqrt(jnp.float32(entries)) / (jnp.sqrt(squares) + 1e-06))
    clipped = clipf * gradient
    first_old = (
        (first_codes.astype(jnp.float32) - 7.5)
        / 7.5
        * jnp.minimum(first_rows[:, None], first_cols[None, :])
    )
    second_level = (second_codes.astype(jnp.float32) + 1.0) / 16.0
    second_old = (
        second_level * second_level * jnp.minimum(second_rows[:, None], second_cols[None, :])
    )
    first_new = 0.9 * first_old + 0.1 * clipped
    second_new = 0.95 * second_old + 0.05 * clipped * clipped
    steps = step_count.astype(jnp.float32)
    first_fix = 1.0 - jnp.power(jnp.float32(0.9), steps)
    second_fix = 1.0 - jnp.power(jnp.float32(0.95), steps)
    update_ratio = first_new / first_fix / (jnp.sqrt(second_new / second_fix) + 1e-08)
    new_master = master_weights - 0.001 * (update_ratio + 0.1 * master_weights)
    gathered_params = whole_of(new_master.astype(jnp.bfloat16), ("dp_0", ("dp_1", "dp_2")), 0)
    first_abs = jnp.abs(first_new)
    first_rowpart = jnp.max(first_abs, axis=1)
    first_colpart = jnp.max(first_abs, axis=0)
    second_rowpart = jnp.max(second_new, axis=1)
    second_colpart = jnp.max(second_new, axis=0)
    new_first_rows, new_second_rows = in_one((first_rowpart, second_rowpart), MP)
    new_first_cols, new_second_cols = together(
        (first_colpart, second_colpart), (("dp_0", "dp_1"), "dp_2")
    )
    first_scaled = first_new / (
        jnp.minimum(new_first_rows[:, None], new_first_cols[None, :]) + 1e-08
    )
    second_scaled = second_new / (
        jnp.minimum(new_second_rows[:, None], new_second_cols[None, :]) + 1e-08
    )
    return (
        new_master,
        update_ratio,
        gathered_params,
        first_scaled,
        second_scaled,
        new_first_rows,
        new_first_cols,
        new_second_rows,
        new_second_cols,
    )


def solution(mesh):
    finer = Mesh(mesh.devices.reshape(2, 8, 8, 2, 2), ("dp_0", "dp_1", "dp_2", "mp_0", "mp_1"))
    in_specs = (
        P(DP, None),
        P(DP, MP),
        P(DP, MP),
        P(DP, MP),
        P(DP, MP),
        P(DP),
        P(MP),
        P(DP),
        P(MP),
        P(),
    )
    out_specs = (
        P(DP, MP),
        P(DP, MP),
        P(None, MP),
        P(DP, MP),
        P(DP, MP),
        P(DP),
        P(MP),
        P(DP),
        P(MP),
    )
    return jax.shard_map(
        shards, mesh=finer, in_specs=in_specs, out_specs=out_specs, check_vma=False
    )
```

profile of v0, /device:TPU:6, one launch (start us, length us, event | category | flops | bytes accessed | tf_op | source)
XLA Modules:
  0.0 267.6 jit_solution(6293149724688112334)
XLA Ops:
  0.7 1.1 copy-done
  1.8 4.0 %fusion.6 = f32[384,2048]{1,0:T(8,128)S(1)} fusion(bf16[1024,384]{1,0:T(8,128)(2,1)S(1)} %copy-done, bf16[1024,2048]{1,0:T(8,128)(2,1)} %param.11), kind=kOutput, calls=%fused_computation.16 | convolution fusion | flops 1610612736 | bytes 8126464 | tf_op jit(solution)/shard_map/dot_general | solution.py:94
  5.8 39.0 %all_to_all.38 = f32[2,192,2048]{2,1,0:T(8,128)} all-to-all(f32[2,192,2048]{2,1,0:T(8,128)S(1)} %bitcast.4), channel_id=1, replica_groups=mesh['dp_0'=2,'dp_1'=8,'dp_2'=8,'mp_0'=2,'mp_1'=2] {'dp_0'}, dimensions={0} | all-to-all | bytes 6291456 | tf_op jit(solution)/shard_map/all_to_all | solution.py:21
  44.9 3.4 %reduce_sum.27 = f32[192,2048]{1,0:T(8,128)} reduce(f32[2,192,2048]{2,1,0:T(8,128)} %all_to_all.38, f32[]{:T(128)} %constant.5.clone.1), dimensions={0}, to_apply=%region_0.0 | reduce | flops 393216 | bytes 4718596 | tf_op jit(solution)/shard_map/reduce_sum | solution.py:22
  48.3 2.5 reshape.45
  50.9 69.1 %all_to_all.39 = f32[64,3,2048]{2,1,0:T(4,128)} all-to-all(f32[64,3,2048]{2,1,0:T(4,128)S(1)} %reshape.45), channel_id=1, replica_groups=mesh['dp_0'=2,'dp_1'=8,'dp_2'=8,'mp_0'=2,'mp_1'=2] {'dp_1','dp_2'}, dimensions={0} | all-to-all | bytes 3145728 | tf_op jit(solution)/shard_map/all_to_all | solution.py:21
  120.0 1.9 reduce_sum.28
  122.5 5.5 %psum.35 = f32[]{:T(128)} all-reduce(f32[]{:T(128)} %multiply_reduce_fusion), channel_id=1, replica_groups=mesh['dp_0'=2,'dp_1'=8,'dp_2'=8,'mp_0'=2,'mp_1'=2] {'dp_0'}, use_global_device_ids=true, to_apply=%region_3.0 | all-reduce | flops 1 | bytes 8 | tf_op jit(solution)/shard_map/psum | solution.py:32
  128.0 16.3 %psum.36 = f32[]{:T(128)} all-reduce(f32[]{:T(128)} %psum.35), channel_id=1, replica_groups=mesh['dp_0'=2,'dp_1'=8,'dp_2'=8,'mp_0'=2,'mp_1'=2] {'dp_1'}, use_global_device_ids=true, to_apply=%region_4.0 | all-reduce | flops 1 | bytes 8 | tf_op jit(solution)/shard_map/psum | solution.py:32
  144.4 15.6 %psum.37 = f32[]{:T(128)} all-reduce(f32[]{:T(128)} %psum.36), channel_id=1, replica_groups=mesh['dp_0'=2,'dp_1'=8,'dp_2'=8,'mp_0'=2,'mp_1'=2] {'dp_2'}, use_global_device_ids=true, to_apply=%region_5.0 | all-reduce | flops 1 | bytes 8 | tf_op jit(solution)/shard_map/psum | solution.py:32
  159.9 7.1 %psum.38 = f32[]{:T(128)} all-reduce(f32[]{:T(128)} %psum.37), channel_id=1, replica_groups=mesh['dp_0'=2,'dp_1'=8,'dp_2'=8,'mp_0'=2,'mp_1'=2] {'mp_0'}, use_global_device_ids=true, to_apply=%region_6.0 | all-reduce | flops 1 | bytes 8 | tf_op jit(solution)/shard_map/psum | solution.py:32
  167.0 3.1 %psum.39 = f32[]{:T(128)} all-reduce(f32[]{:T(128)} %psum.38), channel_id=1, replica_groups=mesh['dp_0'=2,'dp_1'=8,'dp_2'=8,'mp_0'=2,'mp_1'=2] {'mp_1'}, use_global_device_ids=true, to_apply=%region_7.0 | all-reduce | flops 1 | bytes 8 | tf_op jit(solution)/shard_map/psum | solution.py:32
  171.8 6.1 %all-to-all-start.5 = ((f32[8,1,4096]{2,1,0:T(1,128)}), f32[8,1,4096]{2,1,0:T(1,128)S(1)}, u32[]{:S(2)}, u32[]{:S(2)}) async-start(f32[8,1,4096]{2,1,0:T(1,128)} %broadcast_in_dim.26), calls=%async_computation.5 | async-start | bytes 262144 | tf_op jit(solution)/shard_map/all_to_all | solution.py:37
  178.0 9.3 %all-to-all-done.5 = f32[8,1,4096]{2,1,0:T(1,128)S(1)} async-done(((f32[8,1,4096]{2,1,0:T(1,128)}), f32[8,1,4096]{2,1,0:T(1,128)S(1)}, u32[]{:S(2)}, u32[]{:S(2)}) %all-to-all-start.5) | async-done | bytes 131104 | tf_op jit(solution)/shard_map/all_to_all | solution.py:37
  187.9 4.8 %all-to-all-start.4 = ((f32[4,1,6]{2,1,0:T(1,128)}), f32[4,1,6]{2,1,0:T(1,128)S(1)}, u32[]{:S(2)}, u32[]{:S(2)}) async-start(f32[4,1,6]{2,1,0:T(1,128)} %broadcast_in_dim.12), calls=%async_computation.4 | async-start | bytes 4096 | tf_op jit(solution)/shard_map/all_to_all | solution.py:37
  192.8 1.6 all-to-all-done.4
  194.4 0.9 broadcast_in_dim.27
  195.3 5.5 %all-to-all-start.6 = ((f32[16,1,4096]{2,1,0:T(1,128)}), f32[16,1,4096]{2,1,0:T(1,128)S(1)}, u32[]{:S(2)}, u32[]{:S(2)}) async-start(f32[16,1,4096]{2,1,0:T(1,128)} %broadcast_in_dim.27), calls=%async_computation.6 | async-start | bytes 524288 | tf_op jit(solution)/shard_map/all_to_all | solution.py:37
  201.5 8.5 %all-to-all-done.6 = f32[16,1,4096]{2,1,0:T(1,128)S(1)} async-done(((f32[16,1,4096]{2,1,0:T(1,128)}), f32[16,1,4096]{2,1,0:T(1,128)S(1)}, u32[]{:S(2)}, u32[]{:S(2)}) %all-to-all-start.6) | async-done | bytes 262176 | tf_op jit(solution)/shard_map/all_to_all | solution.py:37
  210.3 0.7 fusion.3
  211.5 33.9 %all_to_all.40 = bf16[64,3,2048]{2,1,0:T(4,128)(2,1)S(1)} all-to-all(bf16[64,3,2048]{2,1,0:T(4,128)(2,1)S(1)} %broadcast_in_dim.10), channel_id=1, replica_groups=mesh['dp_0'=2,'dp_1'=8,'dp_2'=8,'mp_0'=2,'mp_1'=2] {'dp_1','dp_2'}, dimensions={0} | all-to-all | bytes 1572864 | tf_op jit(solution)/shard_map/all_to_all | solution.py:37
  246.2 17.5 %all_to_all.41 = bf16[2,64,3,2048]{3,1,2,0:T(8,128)(2,1)S(1)} all-to-all(bf16[2,64,3,2048]{3,1,2,0:T(8,128)(2,1)S(1)} %broadcast_in_dim.11), channel_id=1, replica_groups=mesh['dp_0'=2,'dp_1'=8,'dp_2'=8,'mp_0'=2,'mp_1'=2] {'dp_0'}, dimensions={0} | all-to-all | bytes 3145728 | tf_op jit(solution)/shard_map/all_to_all | solution.py:37
  263.8 1.4 copy.25
  265.1 2.5 reshape_reshape.3
  (37 shorter events, 3.9 us)
Async XLA Ops:
  0.6 1.1 copy-start
  50.8 120.0 %copy-start.1 = (s32[3,2048]{1,0:T(4,128)S(1)}, s32[3,2048]{1,0:T(4,128)}, u32[]{:S(2)}) copy-start(s32[3,2048]{1,0:T(4,128)} %param.14) | copy-start | bytes 73732
  50.8 120.0 %copy-start.2 = (s32[3,2048]{1,0:T(4,128)S(1)}, s32[3,2048]{1,0:T(4,128)}, u32[]{:S(2)}) copy-start(s32[3,2048]{1,0:T(4,128)} %param.13) | copy-start | bytes 73732
  50.8 120.0 %copy-start.6 = (f32[2048]{0:T(1024)S(1)}, f32[2048]{0:T(1024)}, u32[]{:S(2)}) copy-start(f32[2048]{0:T(1024)} %param.18) | copy-start | bytes 24580
  50.8 120.0 %copy-start.7 = (f32[2048]{0:T(1024)S(1)}, f32[2048]{0:T(1024)}, u32[]{:S(2)}) copy-start(f32[2048]{0:T(1024)} %param.16) | copy-start | bytes 24580
  50.8 120.0 %copy-start.10 = (f32[3]{0:T(128)S(1)}, f32[3]{0:T(128)}, u32[]{:S(2)}) copy-start(f32[3]{0:T(128)} %param.17) | copy-start | bytes 40
  50.9 120.0 %copy-start.11 = (f32[3]{0:T(128)S(1)}, f32[3]{0:T(128)}, u32[]{:S(2)}) copy-start(f32[3]{0:T(128)} %param.15) | copy-start | bytes 40
  50.9 159.4 %copy-start.5 = (f32[3,2048]{1,0:T(4,128)S(1)}, f32[3,2048]{1,0:T(4,128)}, u32[]{:S(2)}) copy-start(f32[3,2048]{1,0:T(4,128)} %param.12) | copy-start | bytes 73732
  171.8 15.5 %all-to-all-start.5 = ((f32[8,1,4096]{2,1,0:T(1,128)}), f32[8,1,4096]{2,1,0:T(1,128)S(1)}, u32[]{:S(2)}, u32[]{:S(2)}) async-start(f32[8,1,4096]{2,1,0:T(1,128)} %broadcast_in_dim.26), calls=%async_computation.5 | async-start | bytes 262144 | tf_op jit(solution)/shard_map/all_to_all | solution.py:37
  187.9 6.5 %all-to-all-start.4 = ((f32[4,1,6]{2,1,0:T(1,128)}), f32[4,1,6]{2,1,0:T(1,128)S(1)}, u32[]{:S(2)}, u32[]{:S(2)}) async-start(f32[4,1,6]{2,1,0:T(1,128)} %broadcast_in_dim.12), calls=%async_computation.4 | async-start | bytes 4096 | tf_op jit(solution)/shard_map/all_to_all | solution.py:37
  195.3 14.8 %all-to-all-start.6 = ((f32[16,1,4096]{2,1,0:T(1,128)}), f32[16,1,4096]{2,1,0:T(1,128)S(1)}, u32[]{:S(2)}, u32[]{:S(2)}) async-start(f32[16,1,4096]{2,1,0:T(1,128)} %broadcast_in_dim.27), calls=%async_computation.6 | async-start | bytes 524288 | tf_op jit(solution)/shard_map/all_to_all | solution.py:37
  201.5 44.7 %copy-start.8 = (f32[3]{0:T(128)}, f32[3]{0:T(128)S(1)}, u32[]{:S(2)}) copy-start(f32[3]{0:T(128)S(1)} %get-tuple-element.25) | copy-start | bytes 40
  201.5 44.7 %copy-start.9 = (f32[3]{0:T(128)}, f32[3]{0:T(128)S(1)}, u32[]{:S(2)}) copy-start(f32[3]{0:T(128)S(1)} %get-tuple-element.26) | copy-start | bytes 40
  210.3 35.9 %copy-start.3 = (f32[2048]{0:T(1024)}, f32[2048]{0:T(1024)S(1)}, u32[]{:S(2)}) copy-start(f32[2048]{0:T(1024)S(1)} %get-tuple-element.23) | copy-start | bytes 24580
  210.3 35.9 %copy-start.4 = (f32[2048]{0:T(1024)}, f32[2048]{0:T(1024)S(1)}, u32[]{:S(2)}) copy-start(f32[2048]{0:T(1024)S(1)} %get-tuple-element.24) | copy-start | bytes 24580
where the time goes:
time: 272 us; the launch traced here: 268 us
  blocking collectives  207 us (76%)
  waiting for transfers between devices  19.4 us (7%)
  starting transfers between devices  16.3 us (6%)
  local copies, waits for them, and re-layouts  11.1 us (4%)
  other arithmetic  7.29 us (3%)
  matrix products  4.04 us (1%)
    all_to_all x2, blocking collectives, sum_at_owner(): lax.all_to_all(tiles, axis, split_axis=0, concat_axis=0, tiled=True)  108 us
    all_to_all x2, blocking collectives, sent_to_all(): return lax.all_to_all(copies, axis, split_axis=0, concat_axis=0, tiled=True)  51.4 us
    psum x5, blocking collectives, one_axis_at_a_time(): return functools.reduce(lax.psum, axes, x)  47.6 us
    all_to_all x3, waiting for transfers between devices, sent_to_all(): return lax.all_to_all(copies, axis, split_axis=0, concat_axis=0, tiled=True)  19.4 us
    all_to_all x3, starting transfers between devices, sent_to_all(): return lax.all_to_all(copies, axis, split_axis=0, concat_axis=0, tiled=True)  16.3 us
  transfers between devices with their start and end apart: 3, of which 3 were waited for; matrix products, arithmetic and copies ran while one was open for 0% of the time, Pallas kernels for 0%

commit v1 on v0

v1 whole, which is shorter than its diff:
```python
import jax
import jax.numpy as jnp
import numpy as np
from jax import lax
from jax.experimental import pallas as pl
from jax.experimental.pallas import tpu as pltpu
from jax.sharding import Mesh
from jax.sharding import PartitionSpec as P

DP = ("dp_0", "dp_1", "dp_2")
MP = ("mp_0", "mp_1")
MESH = pl.DeviceIdType.MESH
F32, BF16, I16, I32 = jnp.float32, jnp.bfloat16, jnp.int16, jnp.int32

RING = 8
PLANE = 16
OWN = 3
CHUNK = PLANE * OWN
ROWS = RING * CHUNK
COLS = 2048
WIDTH = 512
BLOCKS = 4
TOKENS = 1024
ORDER = (2, 0, 3, 1)
TOP = 32767.0


def along_y(b):
    return b < 2


def long_way(b):
    return 1 if b % 2 else -1


def kernel(
    hid,
    cot,
    master,
    codes1,
    codes2,
    rows1,
    cols1,
    rows2,
    cols2,
    step,
    perm,
    back_y,
    back_z,
    out_master,
    out_ratio,
    out_params,
    out_scaled1,
    out_scaled2,
    out_rows1,
    out_cols1,
    out_rows2,
    out_cols2,
    hid_v,
    cot_v,
    perm_v,
    back_v,
    hid_t,
    grad,
    ship,
    ship_scale,
    land,
    land_scale,
    total,
    piece_out,
    piece_in,
    norm_out,
    norm_in,
    fresh,
    near,
    join,
    whole,
    natural,
    col_out,
    col_in,
    row_out,
    row_in,
    local_sem,
    out_sem,
    ring_send,
    ring_recv,
    scale_send,
    scale_recv,
    plane_send,
    plane_recv,
    norm_send,
    norm_recv,
    near_send,
    near_recv,
    whole_send,
    whole_recv,
    col_send,
    col_recv,
    row_send,
    row_recv,
):
    xl = lax.axis_index("dp_0")
    z = lax.axis_index("dp_1")
    y = lax.axis_index("dp_2")
    xh = lax.axis_index("mp_0")
    core = lax.axis_index("mp_1")
    plane_z = xl * 8 + z
    plane_y = xl * 8 + y
    cube = xl * 4 + xh * 2 + core
    quad = xh * 2 + core

    def in_plane(b, k):
        return {"dp_0": k // 8, ("dp_1" if along_y(b) else "dp_2"): k % 8}

    def in_plane_z(k):
        return {"dp_0": k // 8, "dp_1": k % 8}

    def my_place(b):
        return plane_z if along_y(b) else plane_y

    def on_ring(b, c):
        return {("dp_2" if along_y(b) else "dp_1"): lax.rem(c + 16, 8)}

    def my_ring(b):
        return y if along_y(b) else z

    def in_cube(k):
        return {"dp_0": k // 4, "mp_0": (k // 2) % 2, "mp_1": k % 2}

    def in_quad(k):
        return {"mp_0": k // 2, "mp_1": k % 2}

    def remote(src, dst, send, recv, where):
        return pltpu.make_async_remote_copy(
            src_ref=src,
            dst_ref=dst,
            send_sem=send,
            recv_sem=recv,
            device_id=where,
            device_id_type=MESH,
        )

    def each_other(count, me, act):
        def body(i, carry):
            act(lax.rem(me + i, count))
            return carry

        lax.fori_loop(1, count, body, 0)

    def bytes_of(ref, sem):
        pltpu.make_async_copy(ref, ref, sem).wait()

    barrier = pltpu.get_barrier_semaphore()

    def greet(where):
        pl.semaphore_signal(barrier, inc=1, device_id=where, device_id_type=MESH)

    each_other(16, plane_z, lambda k: greet(in_plane_z(k)))

    def greet_y(i, carry):
        other = lax.rem(y + i, 8)
        greet({"dp_2": other})
        greet({"dp_0": 1 - xl, "dp_2": other})
        return carry

    lax.fori_loop(1, 8, greet_y, 0)

    def greet_mp(i, carry):
        k = lax.rem(quad + i, 4)
        greet(in_quad(k))
        greet({"dp_0": 1 - xl, "mp_0": k // 2, "mp_1": k % 2})
        return carry

    lax.fori_loop(1, 4, greet_mp, 0)

    hid_copy = pltpu.make_async_copy(hid, hid_v, local_sem.at[4])
    hid_copy.start()
    cot_copies = {}
    for b in ORDER:
        cot_copies[b] = pltpu.make_async_copy(
            cot.at[:, pl.ds(b * WIDTH, WIDTH)], cot_v.at[b], local_sem.at[b]
        )
    cot_copies[ORDER[0]].start()
    perm_copy = pltpu.make_async_copy(perm, perm_v, local_sem.at[5])
    perm_copy.start()
    for b in ORDER[1:]:
        cot_copies[b].start()
    back_copies = [
        pltpu.make_async_copy(back_y, back_v.at[0], local_sem.at[6]),
        pltpu.make_async_copy(back_z, back_v.at[1], local_sem.at[7]),
    ]
    for copy in back_copies:
        copy.start()

    ring_copies = {}

    def send_ring(b, slot, way, value):
        peak = jnp.maximum(jnp.max(jnp.abs(value), axis=0, keepdims=True), 1e-30)
        ship_scale[b, slot] = peak * (1.0 / TOP)
        coded = jnp.round(value * (TOP / peak))
        ship[b, slot] = coded.astype(I32).astype(I16)
        where = on_ring(b, my_ring(b) + way)
        data = remote(
            ship.at[b, slot], land.at[b, slot], ring_send.at[b], ring_recv.at[b, slot], where
        )
        scale = remote(
            ship_scale.at[b, slot],
            land_scale.at[b, slot],
            scale_send.at[b],
            scale_recv.at[b, slot],
            where,
        )
        data.start()
        scale.start()
        ring_copies[b, slot] = (data, scale)

    def arrived(b, slot):
        data, scale = ring_copies[b, slot]
        data.wait_recv()
        scale.wait_recv()
        return land[b, slot].astype(I32).astype(F32) * land_scale[b, slot]

    def own(b, c):
        return grad[b, lax.rem(c + 16, 8)]

    def first_sends(b):
        me, way = my_ring(b), long_way(b)
        send_ring(b, 0, way, own(b, me + 4))
        send_ring(b, 4, -way, own(b, me - 3 * way))

    hid_copy.wait()
    hid_t[1] = hid_v[...].T
    ready = False
    for b in ORDER:
        if b == ORDER[1]:
            perm_copy.wait()
            hid_t[0] = jnp.dot(perm_v[...], hid_t[1], preferred_element_type=F32).astype(BF16)
        cot_copies[b].wait()
        lhs = hid_t[0] if along_y(b) else hid_t[1]
        product = jnp.dot(lhs, cot_v[b], preferred_element_type=F32)
        if along_y(b):
            grad[b] = product.reshape(RING, CHUNK, WIDTH)
        else:
            half = CHUNK // 2
            grad[b, :, 0:half] = product[0 : ROWS // 2].reshape(RING, half, WIDTH)
            grad[b, :, half:CHUNK] = product[ROWS // 2 :].reshape(RING, half, WIDTH)
        if not ready:
            pl.semaphore_wait(barrier, 15 + 14 + 6)
            ready = True
        first_sends(b)

    for s in (1, 2):
        for b in ORDER:
            me, way = my_ring(b), long_way(b)
            send_ring(b, s, way, arrived(b, s - 1) + own(b, me + way * (4 - s)))
            send_ring(b, 4 + s, -way, arrived(b, 3 + s) + own(b, me - way * (3 - s)))
    for b in ORDER:
        me, way = my_ring(b), long_way(b)
        send_ring(b, 3, way, arrived(b, 2) + own(b, me + way))
        total[b] = arrived(b, 6) + own(b, me)
    for b in ORDER:
        total[b] += arrived(b, 3)
        for k in range(PLANE):
            piece_out[b, k] = total[b, OWN * k : OWN * k + OWN]
        mine = my_place(b)
        piece_in[b, mine] = piece_out[b, mine]

        def send_piece(k, b=b, mine=mine):
            remote(
                piece_out.at[b, k],
                piece_in.at[b, mine],
                plane_send.at[b],
                plane_recv.at[b],
                in_plane(b, k),
            ).start()

        each_other(PLANE, mine, send_piece)

    def as_column(ref):
        at = lax.broadcasted_iota(I32, (OWN, 1), 0)
        return jnp.where(at == 0, ref[0], jnp.where(at == 1, ref[1], ref[2]))

    first_old = (
        (codes1[...].astype(F32) - 7.5) / 7.5 * jnp.minimum(as_column(rows1), cols1[...])
    )
    level = (codes2[...].astype(F32) + 1.0) / 16.0
    second_old = level * level * jnp.minimum(as_column(rows2), cols2[...])
    steps = jnp.full((1, 128), step[0].astype(F32))
    first_fix = (1.0 - jnp.exp(steps * np.float32(np.log(0.9))))[:, 0:1]
    second_fix = (1.0 - jnp.exp(steps * np.float32(np.log(0.95))))[:, 0:1]

    parts = []
    for b in ORDER:
        bytes_of(piece_in.at[b, pl.ds(0, PLANE - 1)], plane_recv.at[b])
        parts.append((b, jnp.sum(piece_in[b], axis=0)))
    parts = dict(parts)
    gradient = jnp.concatenate([parts[b] for b in range(BLOCKS)], axis=1)

    square = jnp.sum(jnp.sum(gradient * gradient, axis=1, keepdims=True), axis=0, keepdims=True)
    square = jnp.broadcast_to(square, (1, 128))
    for phase, (me, to) in enumerate(
        ((y, lambda k: {"dp_2": k}), (z, lambda k: {"dp_1": k}), (cube, in_cube))
    ):
        norm_out[phase] = square
        norm_in[phase, me] = square

        def send_norm(k, phase=phase, me=me, to=to):
            remote(
                norm_out.at[phase],
                norm_in.at[phase, me],
                norm_send.at[phase],
                norm_recv.at[phase],
                to(k),
            ).start()

        each_other(8, me, send_norm)
        bytes_of(norm_in.at[phase, pl.ds(0, 7)], norm_recv.at[phase])
        square = jnp.sum(norm_in[phase], axis=0)

    entries = np.float32(3145728.0)
    limit = np.float32(0.01) * np.sqrt(entries)
    clipf = jnp.minimum(1.0, limit / (jnp.sqrt(square) + 1e-06))[:, 0:1]
    clipped = clipf * gradient
    first_new = 0.9 * first_old + 0.1 * clipped
    second_new = 0.95 * second_old + 0.05 * clipped * clipped
    ratio = first_new / first_fix / (jnp.sqrt(second_new / second_fix) + 1e-08)
    new_master = master[...] - 0.001 * (ratio + 0.1 * master[...])
    out_ratio[...] = ratio
    out_master[...] = new_master

    rounded = new_master.astype(BF16)
    for b in ORDER:
        mine = my_place(b)
        fresh[b] = rounded[:, b * WIDTH : (b + 1) * WIDTH]
        near[b, mine] = rounded[:, b * WIDTH : (b + 1) * WIDTH]

        def send_near(k, b=b, mine=mine):
            remote(
                fresh.at[b], near.at[b, mine], near_send.at[b], near_recv.at[b], in_plane(b, k)
            ).start()

        each_other(PLANE, mine, send_near)

    first_abs = jnp.abs(first_new)
    row_out[0] = jnp.broadcast_to(jnp.max(first_abs, axis=1, keepdims=True), (OWN, 128))
    row_out[1] = jnp.broadcast_to(jnp.max(second_new, axis=1, keepdims=True), (OWN, 128))
    row_in[quad] = row_out[...]
    each_other(
        4,
        quad,
        lambda k: remote(row_out, row_in.at[quad], row_send, row_recv, in_quad(k)).start(),
    )
    tops = jnp.concatenate(
        [jnp.max(first_abs, axis=0, keepdims=True), jnp.max(second_new, axis=0, keepdims=True)],
        axis=0,
    )
    for k in range(PLANE):
        col_out[0, k] = tops[:, 128 * k : 128 * k + 128]
    col_in[0, plane_z] = col_out[0, plane_z]
    each_other(
        PLANE,
        plane_z,
        lambda k: remote(
            col_out.at[0, k],
            col_in.at[0, plane_z],
            col_send.at[0],
            col_recv.at[0],
            in_plane_z(k),
        ).start(),
    )

    whole_copies = {}

    def pass_on(b, slot, way, c):
        at = lax.rem(c + 16, 8)
        copy = remote(
            whole.at[b, at],
            whole.at[b, at],
            whole_send.at[b],
            whole_recv.at[b, slot],
            on_ring(b, my_ring(b) + way),
        )
        copy.start()
        whole_copies[b, slot] = copy

    for b in ORDER:
        me, way = my_ring(b), long_way(b)
        bytes_of(near.at[b, pl.ds(0, PLANE - 1)], near_recv.at[b])
        for k in range(PLANE):
            join[b, OWN * k : OWN * k + OWN] = near[b, k].astype(F32)
        whole[b, me] = join[b].astype(BF16)
        pass_on(b, 0, way, me)
        pass_on(b, 4, -way, me)

    bytes_of(col_in.at[0, pl.ds(0, PLANE - 1)], col_recv.at[0])
    best = jnp.max(col_in[0], axis=0)
    col_out[1, 0] = best
    col_in[1, y] = best
    each_other(
        8,
        y,
        lambda k: remote(
            col_out.at[1, 0], col_in.at[1, y], col_send.at[1], col_recv.at[1], {"dp_2": k}
        ).start(),
    )

    def step_on(s):
        for b in ORDER:
            me, way = my_ring(b), long_way(b)
            whole_copies[b, s - 1].wait_recv()
            pass_on(b, s, way, me - way * s)
            if s < 3:
                whole_copies[b, 3 + s].wait_recv()
                pass_on(b, 4 + s, -way, me + way * s)

    step_on(1)
    bytes_of(col_in.at[1, pl.ds(0, 7)], col_recv.at[1])
    best = jnp.max(col_in[1, 0:8], axis=0)
    col_out[2, 0] = best
    col_in[2, plane_z] = best
    each_other(
        PLANE,
        plane_z,
        lambda k: remote(
            col_out.at[2, 0], col_in.at[2, plane_z], col_send.at[2], col_recv.at[2], in_plane_z(k)
        ).start(),
    )
    step_on(2)

    bytes_of(row_in.at[pl.ds(0, 3)], row_recv)
    row_top = jnp.max(row_in[...], axis=0)
    for j in range(OWN):
        out_rows1[j] = jnp.max(row_top[0, j : j + 1])
        out_rows2[j] = jnp.max(row_top[1, j : j + 1])
    step_on(3)

    bytes_of(col_in.at[2, pl.ds(0, PLANE - 1)], col_recv.at[2])
    for k in range(PLANE):
        out_cols1[:, 128 * k : 128 * k + 128] = col_in[2, k, 0:1]
        out_cols2[:, 128 * k : 128 * k + 128] = col_in[2, k, 1:2]
    out_scaled1[...] = first_new / (jnp.minimum(row_top[0, :, 0:1], out_cols1[...]) + 1e-08)
    out_scaled2[...] = second_new / (jnp.minimum(row_top[1, :, 0:1], out_cols2[...]) + 1e-08)

    for copy in back_copies:
        copy.wait()
    out_copies = []
    for b in ORDER:
        whole_copies[b, 3].wait_recv()
        whole_copies[b, 6].wait_recv()
        natural[b] = jnp.dot(
            back_v[0 if along_y(b) else 1],
            whole[b].reshape(ROWS, WIDTH),
            preferred_element_type=F32,
        ).astype(BF16)
        copy = pltpu.make_async_copy(
            natural.at[b], out_params.at[:, pl.ds(b * WIDTH, WIDTH)], out_sem.at[b]
        )
        copy.start()
        out_copies.append(copy)

    for b in range(BLOCKS):
        bytes_of(ship.at[b], ring_send.at[b])
        bytes_of(ship_scale.at[b], scale_send.at[b])
        bytes_of(piece_out.at[b, pl.ds(0, PLANE - 1)], plane_send.at[b])
        bytes_of(near.at[b, pl.ds(0, PLANE - 1)], near_send.at[b])
        bytes_of(whole.at[b, pl.ds(0, 7)], whole_send.at[b])
    for phase in range(3):
        bytes_of(norm_in.at[phase, pl.ds(0, 7)], norm_send.at[phase])
        bytes_of(
            col_in.at[phase, pl.ds(0, 7 if phase == 1 else PLANE - 1)], col_send.at[phase]
        )
    bytes_of(row_in.at[pl.ds(0, 3)], row_send)
    for copy in out_copies:
        copy.wait()


def permutations():
    natural = np.arange(ROWS)
    by_y = natural.reshape(PLANE, RING, OWN).transpose(1, 0, 2).reshape(-1)
    by_z = natural.reshape(2, RING, RING, OWN).transpose(1, 0, 2, 3).reshape(-1)
    to_y = np.zeros((ROWS, ROWS), np.float32)
    to_y[natural, by_y] = 1.0
    to_z = np.zeros((ROWS, ROWS), np.float32)
    to_z[natural, by_z] = 1.0
    return to_y, to_y.T, to_z.T


def shards(
    hidden_input,
    output_cotangent,
    master_weights,
    first_codes,
    second_codes,
    first_rows,
    first_cols,
    second_rows,
    second_cols,
    step_count,
):
    own = jax.ShapeDtypeStruct((OWN, COLS), F32)
    row = jax.ShapeDtypeStruct((OWN,), F32)
    col = jax.ShapeDtypeStruct((1, COLS), F32)
    anywhere = pl.BlockSpec(memory_space=pl.ANY)
    vmem = pl.BlockSpec(memory_space=pltpu.VMEM)
    smem = pl.BlockSpec(memory_space=pltpu.SMEM)
    dma = pltpu.SemaphoreType.DMA
    outs = pl.pallas_call(
        kernel,
        out_shape=(
            own,
            own,
            jax.ShapeDtypeStruct((ROWS, COLS), BF16),
            own,
            own,
            row,
            col,
            row,
            col,
        ),
        in_specs=[
            anywhere,
            anywhere,
            vmem,
            vmem,
            vmem,
            smem,
            vmem,
            smem,
            vmem,
            smem,
            anywhere,
            anywhere,
            anywhere,
        ],
        out_specs=(vmem, vmem, anywhere, vmem, vmem, smem, vmem, smem, vmem),
        scratch_shapes=[
            pltpu.VMEM((TOKENS, ROWS), BF16),
            pltpu.VMEM((BLOCKS, TOKENS, WIDTH), BF16),
            pltpu.VMEM((ROWS, ROWS), BF16),
            pltpu.VMEM((2, ROWS, ROWS), BF16),
            pltpu.VMEM((2, ROWS, TOKENS), BF16),
            pltpu.VMEM((BLOCKS, RING, CHUNK, WIDTH), F32),
            pltpu.VMEM((BLOCKS, 7, CHUNK, WIDTH), I16),
            pltpu.VMEM((BLOCKS, 7, 1, WIDTH), F32),
            pltpu.VMEM((BLOCKS, 7, CHUNK, WIDTH), I16),
            pltpu.VMEM((BLOCKS, 7, 1, WIDTH), F32),
            pltpu.VMEM((BLOCKS, CHUNK, WIDTH), F32),
            pltpu.VMEM((BLOCKS, PLANE, OWN, WIDTH), F32),
            pltpu.VMEM((BLOCKS, PLANE, OWN, WIDTH), F32),
            pltpu.VMEM((3, 1, 128), F32),
            pltpu.VMEM((3, 8, 1, 128), F32),
            pltpu.VMEM((BLOCKS, OWN, WIDTH), BF16),
            pltpu.VMEM((BLOCKS, PLANE, OWN, WIDTH), BF16),
            pltpu.VMEM((BLOCKS, CHUNK, WIDTH), F32),
            pltpu.VMEM((BLOCKS, RING, CHUNK, WIDTH), BF16),
            pltpu.VMEM((BLOCKS, ROWS, WIDTH), BF16),
            pltpu.VMEM((3, PLANE, 2, 128), F32),
            pltpu.VMEM((3, PLANE, 2, 128), F32),
            pltpu.VMEM((2, OWN, 128), F32),
            pltpu.VMEM((4, 2, OWN, 128), F32),
            dma((8,)),
            dma((BLOCKS,)),
            dma((BLOCKS,)),
            dma((BLOCKS, 7)),
            dma((BLOCKS,)),
            dma((BLOCKS, 7)),
            dma((BLOCKS,)),
            dma((BLOCKS,)),
            dma((3,)),
            dma((3,)),
            dma((BLOCKS,)),
            dma((BLOCKS,)),
            dma((BLOCKS,)),
            dma((BLOCKS, 7)),
            dma((3,)),
            dma((3,)),
            dma,
            dma,
        ],
        compiler_params=pltpu.CompilerParams(
            collective_id=0, has_side_effects=True, vmem_limit_bytes=56 * 1024 * 1024
        ),
    )(
        hidden_input,
        output_cotangent,
        master_weights,
        first_codes,
        second_codes,
        first_rows,
        first_cols.reshape(1, -1),
        second_rows,
        second_cols.reshape(1, -1),
        step_count.reshape(1),
        *(jnp.asarray(p, BF16) for p in permutations()),
    )
    outs = list(outs)
    outs[6] = outs[6].reshape(-1)
    outs[8] = outs[8].reshape(-1)
    return tuple(outs)


def solution(mesh):
    finer = Mesh(mesh.devices.reshape(2, 8, 8, 2, 2), ("dp_0", "dp_1", "dp_2", "mp_0", "mp_1"))
    in_specs = (
        P(DP, None),
        P(DP, MP),
        P(DP, MP),
        P(DP, MP),
        P(DP, MP),
        P(DP),
        P(MP),
        P(DP),
        P(MP),
        P(),
    )
    out_specs = (
        P(DP, MP),
        P(DP, MP),
        P(None, MP),
        P(DP, MP),
        P(DP, MP),
        P(DP),
        P(MP),
        P(DP),
        P(MP),
    )
    return jax.shard_map(
        shards, mesh=finer, in_specs=in_specs, out_specs=out_specs, check_vma=False
    )
```

time: 272 us -> 88.7 us (0.33)
  the two profiles are of different devices: /device:TPU:6 before, /device:TPU:2 now
where the time goes in v1:
time: 88.7 us; the launch traced here: 88.4 us
  Pallas kernels  78 us (88%)
  local copies, waits for them, and re-layouts  9 us (10%)
  between operations  1.33 us (1%)
    pallas_call x1, Pallas kernels, shards(): pl.pallas_call(kernel, out_shape=(own, own, jax.ShapeDtypeStruct((ROWS, C...  78 us
    unnamed x21, local copies, waits for them, and re-layouts  9 us

profile of v1, /device:TPU:2, one launch (start us, length us, event | category | flops | bytes accessed | tf_op | source)
XLA Modules:
  0.0 88.4 jit_solution(7660644528615800967)
XLA Ops:
  1.3 78.0 %shard_map.196 = (f32[3,2048]{1,0:T(4,128)}, f32[3,2048]{1,0:T(4,128)}, bf16[384,2048]{1,0:T(8,128)(2,1)}, f32[3,2048]{1,0:T(4,128)}, f32[3,2048]{1,0:T(4,128)},...) custom-call(bf16[1024,384]{1,0:T(8,128)(2,1)} %hid.1, bf16[1024,2048]{1,0:T(8,128)(2,1)} %cot.1, ...), custom_call_target="tpu_custom_call" | custom-call | tf_op jit(solution)/shard_map/pallas_call | solution.py:507
  79.3 1.4 %copy.32 = f32[3,2048]{1,0:T(4,128)} copy(f32[3,2048]{1,0:T(4,128)} %get-tuple-element.36) | data formatting | bytes 49152
  80.7 1.4 %copy.33 = f32[3,2048]{1,0:T(4,128)} copy(f32[3,2048]{1,0:T(4,128)} %get-tuple-element.37) | data formatting | bytes 49152
  82.1 0.0 copy-start.1
  82.1 0.0 copy-start
  82.1 0.0 copy-start.5
  82.1 0.0 copy-start.3
  82.1 0.0 copy-start.4
  82.1 0.0 copy-start.2
  82.1 2.8 %copy.34 = bf16[384,2048]{1,0:T(8,128)(2,1)} copy(bf16[384,2048]{1,0:T(8,128)(2,1)} %get-tuple-element.38) | data formatting | bytes 3145728
  84.9 0.0 copy-done.1
  84.9 0.6 copy.35
  85.5 0.0 copy-done
  85.5 0.6 copy.36
  86.1 0.0 copy-done.5
  86.1 0.5 copy.37
  86.6 0.0 copy-done.3
  86.6 0.6 copy.38
  87.2 0.0 copy-done.4
  87.2 0.5 copy.39
  87.8 0.0 copy-done.2
  87.8 0.6 copy.40
Async XLA Ops:
  82.1 2.8 %copy-start.1 = (f32[3,2048]{1,0:T(4,128)S(1)}, f32[3,2048]{1,0:T(4,128)}, u32[]{:S(2)}) copy-start(f32[3,2048]{1,0:T(4,128)} %get-tuple-element.39) | copy-start | bytes 73732
  82.1 3.4 %copy-start = (f32[3,2048]{1,0:T(4,128)S(1)}, f32[3,2048]{1,0:T(4,128)}, u32[]{:S(2)}) copy-start(f32[3,2048]{1,0:T(4,128)} %get-tuple-element.40) | copy-start | bytes 73732
  82.1 4.0 %copy-start.5 = (f32[3]{0:T(128)S(1)}, f32[3]{0:T(128)}, u32[]{:S(2)}) copy-start(f32[3]{0:T(128)} %get-tuple-element.41) | copy-start | bytes 40
  82.1 4.5 %copy-start.3 = (f32[1,2048]{1,0:T(1,128)S(1)}, f32[1,2048]{1,0:T(1,128)}, u32[]{:S(2)}) copy-start(f32[1,2048]{1,0:T(1,128)} %get-tuple-element.24) | copy-start | bytes 24580
  82.1 5.1 %copy-start.4 = (f32[3]{0:T(128)S(1)}, f32[3]{0:T(128)}, u32[]{:S(2)}) copy-start(f32[3]{0:T(128)} %get-tuple-element.43) | copy-start | bytes 40
  82.1 5.6 %copy-start.2 = (f32[1,2048]{1,0:T(1,128)S(1)}, f32[1,2048]{1,0:T(1,128)}, u32[]{:S(2)}) copy-start(f32[1,2048]{1,0:T(1,128)} %get-tuple-element.26) | copy-start | bytes 24580

commit v2 on v1

v2 whole, which is shorter than its diff:
```python
import jax
import jax.numpy as jnp
import numpy as np
from jax import lax
from jax.experimental import pallas as pl
from jax.experimental.pallas import tpu as pltpu
from jax.sharding import Mesh
from jax.sharding import PartitionSpec as P

DP = ("dp_0", "dp_1", "dp_2")
MP = ("mp_0", "mp_1")
MESH = pl.DeviceIdType.MESH
F32, BF16, I16, I32 = jnp.float32, jnp.bfloat16, jnp.int16, jnp.int32

RING = 8
PLANE = 16
OWN = 3
CHUNK = PLANE * OWN
ROWS = RING * CHUNK
COLS = 2048
WIDTH = 256
BLOCKS = 8
HALF = 1024
PART = 512
PARTS = 4
TOKENS = 1024
TOP = 32767.0


def long_way(b):
    return 1 if b % 2 else -1


def kernel(
    hid,
    cot,
    master,
    codes1,
    codes2,
    rows1,
    cols1,
    rows2,
    cols2,
    step,
    perm,
    out_master,
    out_ratio,
    out_whole,
    out_scaled1,
    out_scaled2,
    out_rows,
    out_cols1,
    out_cols2,
    hid_v,
    cot_v,
    perm_v,
    hid_t,
    grad,
    ship,
    ship_scale,
    land,
    land_scale,
    total,
    piece_out,
    piece_in,
    norm_out,
    norm_in,
    fresh,
    near,
    join,
    whole,
    col_out,
    col_in,
    row_out,
    row_in,
    local_sem,
    out_sem,
    ring_send,
    ring_recv,
    scale_send,
    scale_recv,
    plane_send,
    plane_recv,
    norm_send,
    norm_recv,
    near_send,
    near_recv,
    whole_send,
    whole_recv,
    col_send,
    col_recv,
    row_send,
    row_recv,
):
    xl = lax.axis_index("dp_0")
    z = lax.axis_index("dp_1")
    y = lax.axis_index("dp_2")
    xh = lax.axis_index("mp_0")
    core = lax.axis_index("mp_1")
    me = y + core * (z - y)
    other = z + core * (y - z)
    place = xl * 8 + other
    column = core * 8 + y
    sheet = (xl * 2 + xh) * 8 + z
    quad = xh * 2 + core

    def at(ring, across):
        return {"dp_1": across + core * (ring - across), "dp_2": ring + core * (across - ring)}

    def on_ring(c):
        return at(lax.rem(c + 16, 8), other)

    def in_plane(k):
        return {"dp_0": k // 8, **at(me, k % 8)}

    def in_column(k):
        return {"dp_2": k % 8, "mp_1": k // 8}

    def in_sheet(k):
        return {"dp_0": k // 16, "mp_0": (k // 8) % 2, "dp_1": k % 8}

    def in_quad(k):
        return {"mp_0": k // 2, "mp_1": k % 2}

    def remote(src, dst, send, recv, where):
        return pltpu.make_async_remote_copy(
            src_ref=src,
            dst_ref=dst,
            send_sem=send,
            recv_sem=recv,
            device_id=where,
            device_id_type=MESH,
        )

    def each_other(count, me, act):
        def body(i, carry):
            act(lax.rem(me + i, count))
            return carry

        first = count // 2 + 4 if count > 8 else count // 2
        lax.fori_loop(first, count, body, 0)
        lax.fori_loop(1, first, body, 0)

    def bytes_of(ref, sem):
        pltpu.make_async_copy(ref, ref, sem).wait()

    hid_copy = pltpu.make_async_copy(hid, hid_v, local_sem.at[PARTS])
    hid_copy.start()
    perm_copy = pltpu.make_async_copy(perm.at[core], perm_v, local_sem.at[PARTS + 1])
    perm_copy.start()
    cot_copies = []
    for q in range(PARTS):
        copy = pltpu.make_async_copy(
            cot.at[:, pl.ds(q * PART, PART)], cot_v.at[q], local_sem.at[q]
        )
        copy.start()
        cot_copies.append(copy)

    barrier = pltpu.get_barrier_semaphore()

    def greet(where):
        pl.semaphore_signal(barrier, inc=1, device_id=where, device_id_type=MESH)

    each_other(16, column, lambda k: greet(in_column(k)))
    each_other(32, sheet, lambda k: greet(in_sheet(k)))
    each_other(8, y, lambda k: greet({"dp_0": 1 - xl, "dp_2": k}))
    greet({"mp_0": 1 - xh, "mp_1": 1 - core})

    ring_copies = {}

    def send_ring(b, slot, distance, value):
        peak = jnp.maximum(jnp.max(jnp.abs(value), axis=0, keepdims=True), 1e-30)
        ship_scale[b, slot] = peak * (1.0 / TOP)
        coded = jnp.round(value * (TOP / peak))
        ship[b, slot] = coded.astype(I32).astype(I16)
        where = on_ring(me + distance)
        data = remote(
            ship.at[b, slot], land.at[b, slot], ring_send.at[b], ring_recv.at[b, slot], where
        )
        scale = remote(
            ship_scale.at[b, slot],
            land_scale.at[b, slot],
            scale_send.at[b],
            scale_recv.at[b, slot],
            where,
        )
        data.start()
        scale.start()
        ring_copies[b, slot] = (data, scale)

    def arrived(b, slot):
        data, scale = ring_copies[b, slot]
        data.wait_recv()
        scale.wait_recv()
        return land[b, slot].astype(I32).astype(F32) * land_scale[b, slot]

    def own(b, c):
        return grad[b, lax.rem(c + 16, 8)]

    def first_sends(b):
        way = long_way(b)
        send_ring(b, 6, 2 * way, own(b, me + 4))
        send_ring(b, 0, 1, own(b, me + 3))
        send_ring(b, 3, -1, own(b, me - 3))

    hid_copy.wait()
    perm_copy.wait()
    hid_t[...] = lax.dot_general(
        perm_v[...], hid_v[...], (((1,), (1,)), ((), ())), preferred_element_type=F32
    ).astype(BF16)
    for q in range(PARTS):
        cot_copies[q].wait()
        product = jnp.dot(hid_t[...], cot_v[q], preferred_element_type=F32)
        for b in (2 * q, 2 * q + 1):
            start = (b % 2) * WIDTH
            grad[b] = product[:, start : start + WIDTH].reshape(RING, CHUNK, WIDTH)
        if q == 0:
            pl.semaphore_wait(barrier, 15 + 31 + 7 + 1)
        for b in (2 * q, 2 * q + 1):
            first_sends(b)

    for b in range(BLOCKS):
        far = arrived(b, 6)
        ahead, behind = arrived(b, 0) + own(b, me + 2), arrived(b, 3) + own(b, me - 2)
        if long_way(b) > 0:
            ahead += far
        else:
            behind += far
        send_ring(b, 1, 1, ahead)
        send_ring(b, 4, -1, behind)
    for b in range(BLOCKS):
        send_ring(b, 2, 1, arrived(b, 1) + own(b, me + 1))
        send_ring(b, 5, -1, arrived(b, 4) + own(b, me - 1))
    for h in range(2):
        for i in range(4):
            b = 4 * h + i
            total[h, :, WIDTH * i : WIDTH * (i + 1)] = own(b, me) + arrived(b, 2) + arrived(b, 5)
        value = total[h]
        peak = jnp.maximum(jnp.max(jnp.abs(value), axis=0, keepdims=True), 1e-30)
        power = jnp.floor(jnp.log2(peak)) + 1.0
        total[h] = jnp.round(value * (TOP * jnp.exp2(-power)))
        for k in range(PLANE):
            piece = jnp.concatenate([total[h, OWN * k : OWN * k + OWN], power], axis=0)
            piece_out[h, k] = piece.astype(I32).astype(I16)
        piece_in[h, place] = piece_out[h, place]

        def send_piece(k, h=h):
            remote(
                piece_out.at[h, k],
                piece_in.at[h, place],
                plane_send.at[h],
                plane_recv.at[h],
                in_plane(k),
            ).start()

        each_other(PLANE, place, send_piece)

    def as_column(ref):
        at = lax.broadcasted_iota(I32, (OWN, 1), 0)
        return jnp.where(at == 0, ref[0], jnp.where(at == 1, ref[1], ref[2]))

    first_old = (
        (codes1[...].astype(F32) - 7.5) / 7.5 * jnp.minimum(as_column(rows1), cols1[...])
    )
    level = (codes2[...].astype(F32) + 1.0) / 16.0
    second_old = level * level * jnp.minimum(as_column(rows2), cols2[...])
    steps = jnp.full((1, 128), step[0].astype(F32))
    first_fix = (1.0 - jnp.exp(steps * np.float32(np.log(0.9))))[:, 0:1]
    second_fix = (1.0 - jnp.exp(steps * np.float32(np.log(0.95))))[:, 0:1]

    parts = {}
    for h in range(2):
        bytes_of(piece_in.at[h, pl.ds(0, PLANE - 1)], plane_recv.at[h])
        parts[h] = jnp.zeros((OWN, HALF), F32)
        for k in range(PLANE):
            piece = piece_in[h, k].astype(I32).astype(F32)
            unit = jnp.exp2(piece[OWN : OWN + 1]) * (1.0 / TOP)
            parts[h] = parts[h] + piece[0:OWN] * unit
    gradient = jnp.concatenate([parts[0], parts[1]], axis=1)

    square = jnp.sum(jnp.sum(gradient * gradient, axis=1, keepdims=True), axis=0, keepdims=True)
    square = jnp.broadcast_to(square, (1, 128))
    for phase, (count, mine, to) in enumerate(((16, column, in_column), (32, sheet, in_sheet))):
        norm_out[phase] = square
        norm_in[phase, mine] = square

        def send_norm(k, phase=phase, mine=mine, to=to):
            remote(
                norm_out.at[phase],
                norm_in.at[phase, mine],
                norm_send.at[phase],
                norm_recv.at[phase],
                to(k),
            ).start()

        each_other(count, mine, send_norm)
        bytes_of(norm_in.at[phase, pl.ds(0, count - 1)], norm_recv.at[phase])
        square = jnp.sum(norm_in[phase, 0:count], axis=0)

    entries = np.float32(3145728.0)
    limit = np.float32(0.01) * np.sqrt(entries)
    clipf = jnp.minimum(1.0, limit / (jnp.sqrt(square) + 1e-06))[:, 0:1]
    clipped = clipf * gradient
    first_new = 0.9 * first_old + 0.1 * clipped
    second_new = 0.95 * second_old + 0.05 * clipped * clipped
    ratio = first_new / first_fix / (jnp.sqrt(second_new / second_fix) + 1e-08)
    new_master = master[...] - 0.001 * (ratio + 0.1 * master[...])
    out_ratio[...] = ratio
    out_master[...] = new_master

    rounded = new_master.astype(BF16)
    for h in range(2):
        fresh[h] = rounded[:, h * HALF : (h + 1) * HALF]
        near[h, place] = rounded[:, h * HALF : (h + 1) * HALF]

        def send_near(k, h=h):
            remote(
                fresh.at[h], near.at[h, place], near_send.at[h], near_recv.at[h], in_plane(k)
            ).start()

        each_other(PLANE, place, send_near)

    first_abs = jnp.abs(first_new)
    row_out[0] = jnp.broadcast_to(jnp.max(first_abs, axis=1, keepdims=True), (OWN, 128))
    row_out[1] = jnp.broadcast_to(jnp.max(second_new, axis=1, keepdims=True), (OWN, 128))
    row_in[quad] = row_out[...]
    each_other(
        4,
        quad,
        lambda k: remote(row_out, row_in.at[quad], row_send, row_recv, in_quad(k)).start(),
    )
    tops = jnp.concatenate(
        [jnp.max(first_abs, axis=0, keepdims=True), jnp.max(second_new, axis=0, keepdims=True)],
        axis=0,
    )
    for k in range(PLANE):
        col_out[0, k] = tops[:, 128 * k : 128 * k + 128]
    col_in[0, place] = col_out[0, place]
    each_other(
        PLANE,
        place,
        lambda k: remote(
            col_out.at[0, k],
            col_in.at[0, place],
            col_send.at[0],
            col_recv.at[0],
            in_plane(k),
        ).start(),
    )

    whole_copies = {}

    def pass_on(b, slot, distance, c):
        at = lax.rem(c + 16, 8)
        copy = remote(
            whole.at[b, at],
            whole.at[b, at],
            whole_send.at[b],
            whole_recv.at[b, slot],
            on_ring(me + distance),
        )
        copy.start()
        whole_copies[b, slot] = copy

    for h in range(2):
        bytes_of(near.at[h, pl.ds(0, PLANE - 1)], near_recv.at[h])
        for k in range(PLANE):
            join[h, OWN * k : OWN * k + OWN] = near[h, k].astype(F32)
        for i in range(4):
            b = 4 * h + i
            whole[b, me] = join[h, :, WIDTH * i : WIDTH * (i + 1)].astype(BF16)
            pass_on(b, 0, 1, me)
            pass_on(b, 3, -1, me)

    bytes_of(col_in.at[0, pl.ds(0, PLANE - 1)], col_recv.at[0])
    best = jnp.max(col_in[0], axis=0)
    col_out[1, 0] = best
    col_in[1, me] = best
    each_other(
        RING,
        me,
        lambda c: remote(
            col_out.at[1, 0], col_in.at[1, me], col_send.at[1], col_recv.at[1], on_ring(c)
        ).start(),
    )

    def step_on(s):
        for b in range(BLOCKS):
            way = long_way(b)
            for first, direction in ((0, 1), (3, -1)):
                whole_copies[b, first + s - 1].wait_recv()
                if s == 2 and direction == way:
                    pass_on(b, 6, 2 * way, me - 2 * way)
                pass_on(b, first + s, direction, me - direction * s)

    step_on(1)
    step_on(2)

    bytes_of(col_in.at[1, pl.ds(0, 7)], col_recv.at[1])
    best = jnp.max(col_in[1, 0:8], axis=0)
    col_out[2, 0] = best
    col_in[2, place] = best
    each_other(
        PLANE,
        place,
        lambda k: remote(
            col_out.at[2, 0], col_in.at[2, place], col_send.at[2], col_recv.at[2], in_plane(k)
        ).start(),
    )
    bytes_of(row_in.at[pl.ds(0, 3)], row_recv)
    row_top = jnp.max(row_in[...], axis=0)
    out_rows[...] = row_top

    out_copies = []
    for b in range(BLOCKS):
        for slot in (2, 5, 6):
            whole_copies[b, slot].wait_recv()
        copy = pltpu.make_async_copy(whole.at[b], out_whole.at[b], out_sem.at[b])
        copy.start()
        out_copies.append(copy)

    bytes_of(col_in.at[2, pl.ds(0, PLANE - 1)], col_recv.at[2])
    for k in range(PLANE):
        out_cols1[:, 128 * k : 128 * k + 128] = col_in[2, k, 0:1]
        out_cols2[:, 128 * k : 128 * k + 128] = col_in[2, k, 1:2]
    out_scaled1[...] = first_new / (jnp.minimum(row_top[0, :, 0:1], out_cols1[...]) + 1e-08)
    out_scaled2[...] = second_new / (jnp.minimum(row_top[1, :, 0:1], out_cols2[...]) + 1e-08)

    for b in range(BLOCKS):
        bytes_of(ship.at[b], ring_send.at[b])
        bytes_of(ship_scale.at[b], scale_send.at[b])
        bytes_of(whole.at[b, pl.ds(0, 7)], whole_send.at[b])
    for h in range(2):
        bytes_of(piece_out.at[h, pl.ds(0, PLANE - 1)], plane_send.at[h])
        bytes_of(near.at[h, pl.ds(0, PLANE - 1)], near_send.at[h])
    for phase in range(2):
        bytes_of(norm_in.at[phase, pl.ds(0, 31 if phase else 15)], norm_send.at[phase])
    for phase in range(3):
        bytes_of(
            col_in.at[phase, pl.ds(0, 7 if phase == 1 else PLANE - 1)], col_send.at[phase]
        )
    bytes_of(row_in.at[pl.ds(0, 3)], row_send)
    for copy in out_copies:
        copy.wait()


def finish(
    whole,
    master,
    ratio,
    scaled1,
    scaled2,
    rows,
    cols1,
    cols2,
    back,
    out_master,
    out_ratio,
    out_params,
    out_scaled1,
    out_scaled2,
    out_rows1,
    out_cols1,
    out_rows2,
    out_cols2,
    whole_v,
    back_v,
    natural,
    own_v,
    col_v,
    row_v,
    in_sem,
    out_sem,
    own_sem,
):
    back_load = pltpu.make_async_copy(
        back.at[lax.axis_index("mp_1")], back_v, own_sem.at[7]
    )
    back_load.start()
    loads = [
        pltpu.make_async_copy(whole.at[b], whole_v.at[b], in_sem.at[b]) for b in range(BLOCKS)
    ]
    for copy in loads:
        copy.start()
    sources = (master, ratio, scaled1, scaled2)
    targets = (out_master, out_ratio, out_scaled1, out_scaled2)
    row_load = pltpu.make_async_copy(rows, row_v, own_sem.at[6])
    row_load.start()
    small = []
    for i in range(4):
        small.append((sources[i], own_v.at[i], targets[i], i))
    small.append((cols1, col_v.at[0], out_cols1, 4))
    small.append((cols2, col_v.at[1], out_cols2, 5))
    ins = [pltpu.make_async_copy(src, at, own_sem.at[i]) for src, at, _, i in small]
    for copy in ins:
        copy.start()
    outs = []
    back_load.wait()
    for q in range(PARTS):
        loads[2 * q].wait()
        loads[2 * q + 1].wait()
        part = jnp.concatenate(
            [whole_v[2 * q].reshape(ROWS, WIDTH), whole_v[2 * q + 1].reshape(ROWS, WIDTH)], axis=1
        )
        natural[q] = jnp.dot(back_v[...], part, preferred_element_type=F32).astype(BF16)
        copy = pltpu.make_async_copy(
            natural.at[q], out_params.at[:, pl.ds(q * PART, PART)], out_sem.at[q]
        )
        copy.start()
        outs.append(copy)
        if q == 0:
            row_load.wait()
            for j in range(OWN):
                out_rows1[j] = jnp.max(row_v[0, j : j + 1])
                out_rows2[j] = jnp.max(row_v[1, j : j + 1])
            for load, (_, at, target, i) in zip(ins, small, strict=True):
                load.wait()
                copy = pltpu.make_async_copy(at, target, own_sem.at[i])
                copy.start()
                outs.append(copy)
    for copy in outs:
        copy.wait()


def permutations():
    natural = np.arange(ROWS)
    by_y = natural.reshape(PLANE, RING, OWN).transpose(1, 0, 2).reshape(-1)
    by_z = natural.reshape(2, RING, RING, OWN).transpose(1, 0, 2, 3).reshape(-1)
    to_y = np.zeros((ROWS, ROWS), np.float32)
    to_y[natural, by_y] = 1.0
    to_z = np.zeros((ROWS, ROWS), np.float32)
    to_z[natural, by_z] = 1.0
    there = np.stack([to_y, to_z])
    return there, there.transpose(0, 2, 1)


def shards(
    hidden_input,
    output_cotangent,
    master_weights,
    first_codes,
    second_codes,
    first_rows,
    first_cols,
    second_rows,
    second_cols,
    step_count,
):
    own = jax.ShapeDtypeStruct((OWN, COLS), F32)
    row = jax.ShapeDtypeStruct((OWN,), F32)
    col = jax.ShapeDtypeStruct((1, COLS), F32)
    anywhere = pl.BlockSpec(memory_space=pl.ANY)
    hbm = pl.BlockSpec(memory_space=pltpu.HBM)
    vmem = pl.BlockSpec(memory_space=pltpu.VMEM)
    smem = pl.BlockSpec(memory_space=pltpu.SMEM)
    dma = pltpu.SemaphoreType.DMA
    perm, back = (jnp.asarray(p, BF16) for p in permutations())
    new_master, ratio, whole, scaled1, scaled2, rows, cols1, cols2 = pl.pallas_call(
        kernel,
        out_shape=(
            own,
            own,
            jax.ShapeDtypeStruct((BLOCKS, RING, CHUNK, WIDTH), BF16),
            own,
            own,
            jax.ShapeDtypeStruct((2, OWN, 128), F32),
            col,
            col,
        ),
        in_specs=[hbm, hbm, vmem, vmem, vmem, smem, vmem, smem, vmem, smem, hbm],
        out_specs=(vmem, vmem, anywhere, vmem, vmem, vmem, vmem, vmem),
        scratch_shapes=[
            pltpu.VMEM((TOKENS, ROWS), BF16),
            pltpu.VMEM((PARTS, TOKENS, PART), BF16),
            pltpu.VMEM((ROWS, ROWS), BF16),
            pltpu.VMEM((ROWS, TOKENS), BF16),
            pltpu.VMEM((BLOCKS, RING, CHUNK, WIDTH), F32),
            pltpu.VMEM((BLOCKS, 7, CHUNK, WIDTH), I16),
            pltpu.VMEM((BLOCKS, 7, 1, WIDTH), F32),
            pltpu.VMEM((BLOCKS, 7, CHUNK, WIDTH), I16),
            pltpu.VMEM((BLOCKS, 7, 1, WIDTH), F32),
            pltpu.VMEM((2, CHUNK, HALF), F32),
            pltpu.VMEM((2, PLANE, OWN + 1, HALF), I16),
            pltpu.VMEM((2, PLANE, OWN + 1, HALF), I16),
            pltpu.VMEM((2, 1, 128), F32),
            pltpu.VMEM((2, 32, 1, 128), F32),
            pltpu.VMEM((2, OWN, HALF), BF16),
            pltpu.VMEM((2, PLANE, OWN, HALF), BF16),
            pltpu.VMEM((2, CHUNK, HALF), F32),
            pltpu.VMEM((BLOCKS, RING, CHUNK, WIDTH), BF16),
            pltpu.VMEM((3, PLANE, 2, 128), F32),
            pltpu.VMEM((3, PLANE, 2, 128), F32),
            pltpu.VMEM((2, OWN, 128), F32),
            pltpu.VMEM((4, 2, OWN, 128), F32),
            dma((PARTS + 2,)),
            dma((BLOCKS,)),
            dma((BLOCKS,)),
            dma((BLOCKS, 7)),
            dma((BLOCKS,)),
            dma((BLOCKS, 7)),
            dma((2,)),
            dma((2,)),
            dma((3,)),
            dma((3,)),
            dma((2,)),
            dma((2,)),
            dma((BLOCKS,)),
            dma((BLOCKS, 7)),
            dma((3,)),
            dma((3,)),
            dma,
            dma,
        ],
        compiler_params=pltpu.CompilerParams(
            collective_id=0, has_side_effects=True, vmem_limit_bytes=60 * 1024 * 1024
        ),
    )(
        hidden_input,
        output_cotangent,
        master_weights,
        first_codes,
        second_codes,
        first_rows,
        first_cols.reshape(1, -1),
        second_rows,
        second_cols.reshape(1, -1),
        step_count.reshape(1),
        perm,
    )
    outs = pl.pallas_call(
        finish,
        out_shape=(
            own,
            own,
            jax.ShapeDtypeStruct((ROWS, COLS), BF16),
            own,
            own,
            row,
            col,
            row,
            col,
        ),
        in_specs=[anywhere] * 8 + [hbm],
        out_specs=(hbm, hbm, hbm, hbm, hbm, smem, hbm, smem, hbm),
        scratch_shapes=[
            pltpu.VMEM((BLOCKS, RING, CHUNK, WIDTH), BF16),
            pltpu.VMEM((ROWS, ROWS), BF16),
            pltpu.VMEM((PARTS, ROWS, PART), BF16),
            pltpu.VMEM((4, OWN, COLS), F32),
            pltpu.VMEM((2, 1, COLS), F32),
            pltpu.VMEM((2, OWN, 128), F32),
            dma((BLOCKS,)),
            dma((BLOCKS,)),
            dma((8,)),
        ],
        compiler_params=pltpu.CompilerParams(vmem_limit_bytes=60 * 1024 * 1024),
    )(whole, new_master, ratio, scaled1, scaled2, rows, cols1, cols2, back)
    outs = list(outs)
    outs[6] = outs[6].reshape(-1)
    outs[8] = outs[8].reshape(-1)
    return tuple(outs)


def solution(mesh):
    finer = Mesh(mesh.devices.reshape(2, 8, 8, 2, 2), ("dp_0", "dp_1", "dp_2", "mp_0", "mp_1"))
    in_specs = (
        P(DP, None),
        P(DP, MP),
        P(DP, MP),
        P(DP, MP),
        P(DP, MP),
        P(DP),
        P(MP),
        P(DP),
        P(MP),
        P(),
    )
    out_specs = (
        P(DP, MP),
        P(DP, MP),
        P(None, MP),
        P(DP, MP),
        P(DP, MP),
        P(DP),
        P(MP),
        P(DP),
        P(MP),
    )
    return jax.shard_map(
        shards, mesh=finer, in_specs=in_specs, out_specs=out_specs, check_vma=False
    )
```

time: 88.7 us -> 79.2 us (0.89)
  the two profiles are of different devices: /device:TPU:2 before, /device:TPU:6 now
where the time goes in v2:
time: 79.2 us; the launch traced here: 78.8 us
  Pallas kernels  77.5 us (98%)
  between operations  1.3 us (2%)
    pallas_call x1, Pallas kernels, shards(): pl.pallas_call(kernel, out_shape=(own, own, jax.ShapeDtypeStruct((BLOCKS,...  73.2 us
    pallas_call x1, Pallas kernels, shards(): pl.pallas_call(finish, out_shape=(own, own, jax.ShapeDtypeStruct((ROWS, C...  4.28 us

profile of v2, /device:TPU:6, one launch (start us, length us, event | category | flops | bytes accessed | tf_op | source)
XLA Modules:
  0.0 78.8 jit_solution(10632214607826196145)
XLA Ops:
  1.3 73.2 %shard_map.187 = (f32[3,2048]{1,0:T(4,128)}, f32[3,2048]{1,0:T(4,128)}, bf16[8,8,48,256]{3,2,1,0:T(8,128)(2,1)}, f32[3,2048]{1,0:T(4,128)}, f32[3,2048]{1,0:T(4,...) custom-call(bf16[1024,384]{1,0:T(8,128)(2,1)} %hid.1, bf16[1024,2048]{1,0:T(8,128)(2,1)} %cot.1, ...), custom_call_target="tpu_custom_call" | custom-call | tf_op jit(solution)/shard_map/pallas_call | solution.py:558
  74.5 4.3 %shard_map.188 = (f32[3,2048]{1,0:T(4,128)}, f32[3,2048]{1,0:T(4,128)}, bf16[384,2048]{1,0:T(8,128)(2,1)}, f32[3,2048]{1,0:T(4,128)}, f32[3,2048]{1,0:T(4,128)},...) custom-call(bf16[8,8,48,256]{3,2,1,0:T(8,128)(2,1)} %get-tuple-element.26.whole, ...), custom_call_target="tpu_custom_call" | custom-call | tf_op jit(solution)/shard_map/pallas_call | solution.py:630

commit v3 on v2

--- a/solution.py
+++ b/solution.py
@@ -18,17 +18,21 @@
 CHUNK = PLANE * OWN
 ROWS = RING * CHUNK
 COLS = 2048
-WIDTH = 256
-BLOCKS = 8
+WIDTH = 512
+BLOCKS = 4
 HALF = 1024
-PART = 512
-PARTS = 4
 TOKENS = 1024
 TOP = 32767.0
+NEED = (4, 3, -3, 2, -2, 1, -1, 0)
+FAR = 3
 
 
 def long_way(b):
     return 1 if b % 2 else -1
+
+
+def steps_of(b):
+    return 4 if b < BLOCKS // 2 else 3
 
 
 def kernel(
@@ -43,17 +47,28 @@
     cols2,
     step,
     perm,
+    back,
     out_master,
     out_ratio,
-    out_whole,
+    out_natural,
     out_scaled1,
     out_scaled2,
     out_rows,
     out_cols1,
     out_cols2,
+    master_v,
+    codes_v,
+    cols_v,
+    rows1_s,
+    rows2_s,
+    step_s,
+    result_v,
+    row_result,
+    col_result,
     hid_v,
     cot_v,
     perm_v,
+    back_v,
     hid_t,
     grad,
     ship,
@@ -69,11 +84,16 @@
     near,
     join,
     whole,
+    natural,
     col_out,
     col_in,
     row_out,
     row_in,
+    news,
+    input_sem,
+    result_sem,
     local_sem,
+    perm_sem,
     out_sem,
     ring_send,
     ring_recv,
@@ -138,33 +158,63 @@
             return carry
 
         first = count // 2 + 4 if count > 8 else count // 2
-        lax.fori_loop(first, count, body, 0)
-        lax.fori_loop(1, first, body, 0)
+        lax.fori_loop(first, count, body, 0, unroll=4)
+        lax.fori_loop(1, first, body, 0, unroll=4)
 
     def bytes_of(ref, sem):
         pltpu.make_async_copy(ref, ref, sem).wait()
 
-    hid_copy = pltpu.make_async_copy(hid, hid_v, local_sem.at[PARTS])
+    hid_copy = pltpu.make_async_copy(hid, hid_v, local_sem.at[BLOCKS])
     hid_copy.start()
-    perm_copy = pltpu.make_async_copy(perm.at[core], perm_v, local_sem.at[PARTS + 1])
+    perm_copy = pltpu.make_async_copy(perm.at[core], perm_v, perm_sem)
     perm_copy.start()
     cot_copies = []
-    for q in range(PARTS):
+    for q in range(BLOCKS):
         copy = pltpu.make_async_copy(
-            cot.at[:, pl.ds(q * PART, PART)], cot_v.at[q], local_sem.at[q]
+            cot.at[:, pl.ds(q * WIDTH, WIDTH)], cot_v.at[q], local_sem.at[q]
         )
-        copy.start()
         cot_copies.append(copy)
+    cot_copies[0].start()
+    back_copy = pltpu.make_async_copy(back.at[core], back_v, local_sem.at[BLOCKS + 1])
+    inputs = (
+        (master, master_v),
+        (codes1, codes_v.at[0]),
+        (codes2, codes_v.at[1]),
+        (cols1, cols_v.at[0]),
+        (cols2, cols_v.at[1]),
+        (rows1, rows1_s),
+        (rows2, rows2_s),
+        (step, step_s),
+    )
+    input_copies = [
+        pltpu.make_async_copy(src, dst, input_sem.at[i]) for i, (src, dst) in enumerate(inputs)
+    ]
 
     barrier = pltpu.get_barrier_semaphore()
 
     def greet(where):
         pl.semaphore_signal(barrier, inc=1, device_id=where, device_id_type=MESH)
 
-    each_other(16, column, lambda k: greet(in_column(k)))
-    each_other(32, sheet, lambda k: greet(in_sheet(k)))
-    each_other(8, y, lambda k: greet({"dp_0": 1 - xl, "dp_2": k}))
-    greet({"mp_0": 1 - xh, "mp_1": 1 - core})
+    for distance in (2, -2, 1, -1):
+        greet(on_ring(me + distance))
+    for distance in (1, -1):
+        across = at(me, lax.rem(other + distance + 8, 8))
+        greet(across)
+        greet({"dp_0": 1 - xl, **across})
+    greet({"dp_0": 1 - xl})
+    each_other(4, quad, lambda k: greet(in_quad(k)))
+
+    def tell(i):
+        for distance in (1, -1):
+            pl.semaphore_signal(
+                news.at[i],
+                inc=1,
+                device_id=at(me, lax.rem(other + distance + 8, 8)),
+                device_id_type=MESH,
+            )
+
+    def hear(i):
+        pl.semaphore_wait(news.at[i], 2)
 
     ring_copies = {}
 
@@ -194,47 +244,82 @@
         scale.wait_recv()
         return land[b, slot].astype(I32).astype(F32) * land_scale[b, slot]
 
-    def own(b, c):
-        return grad[b, lax.rem(c + 16, 8)]
+    def own(b, distance):
+        return grad[b, NEED.index(distance)]
+
+    def slots(b):
+        return (0, 3) if long_way(b) > 0 else (3, 0)
 
     def first_sends(b):
         way = long_way(b)
-        send_ring(b, 6, 2 * way, own(b, me + 4))
-        send_ring(b, 0, 1, own(b, me + 3))
-        send_ring(b, 3, -1, own(b, me - 3))
+        long, short = slots(b)
+        send_ring(b, 6, way if steps_of(b) == 4 else 2 * way, own(b, 4))
+        if steps_of(b) == 3:
+            send_ring(b, long, way, own(b, 3 * way))
+        send_ring(b, short, -way, own(b, -3 * way))
 
     hid_copy.wait()
     perm_copy.wait()
+    for copy in (*cot_copies[1:], *input_copies, back_copy):
+        copy.start()
     hid_t[...] = lax.dot_general(
-        perm_v[...], hid_v[...], (((1,), (1,)), ((), ())), preferred_element_type=F32
+        perm_v[...],
+        hid_v[...],
+        (((1,), (1,)), ((), ())),
+        preferred_element_type=F32,
     ).astype(BF16)
-    for q in range(PARTS):
-        cot_copies[q].wait()
-        product = jnp.dot(hid_t[...], cot_v[q], preferred_element_type=F32)
-        for b in (2 * q, 2 * q + 1):
-            start = (b % 2) * WIDTH
-            grad[b] = product[:, start : start + WIDTH].reshape(RING, CHUNK, WIDTH)
-        if q == 0:
-            pl.semaphore_wait(barrier, 15 + 31 + 7 + 1)
-        for b in (2 * q, 2 * q + 1):
-            first_sends(b)
+
+    def multiply(b, first, last):
+        lhs = jnp.concatenate(
+            [
+                hid_t[pl.ds(pl.multiple_of(lax.rem(me + d + 8, 8) * CHUNK, CHUNK), CHUNK)]
+                for d in NEED[first:last]
+            ],
+            axis=0,
+        )
+        product = jnp.dot(lhs, cot_v[b], preferred_element_type=F32)
+        grad[b, first:last] = product.reshape(last - first, CHUNK, WIDTH)
 
     for b in range(BLOCKS):
+        cot_copies[b].wait()
+        multiply(b, 0, FAR)
+        if b == 0:
+            pl.semaphore_wait(barrier, 4 + 4 + 1 + 3)
+            tell(0)
+        first_sends(b)
+    for b in range(BLOCKS):
+        multiply(b, FAR, RING)
+    hear(0)
+    tell(1)
+
+    for b in range(BLOCKS):
+        way = long_way(b)
+        long, short = slots(b)
         far = arrived(b, 6)
-        ahead, behind = arrived(b, 0) + own(b, me + 2), arrived(b, 3) + own(b, me - 2)
-        if long_way(b) > 0:
-            ahead += far
+        if steps_of(b) == 4:
+            send_ring(b, long, way, far + own(b, 3 * way))
         else:
-            behind += far
-        send_ring(b, 1, 1, ahead)
-        send_ring(b, 4, -1, behind)
+            send_ring(b, long + 1, way, far + arrived(b, long) + own(b, 2 * way))
+        send_ring(b, short + 1, -way, arrived(b, short) + own(b, -2 * way))
+    hear(1)
+    tell(2)
     for b in range(BLOCKS):
-        send_ring(b, 2, 1, arrived(b, 1) + own(b, me + 1))
-        send_ring(b, 5, -1, arrived(b, 4) + own(b, me - 1))
-    for h in range(2):
-        for i in range(4):
-            b = 4 * h + i
-            total[h, :, WIDTH * i : WIDTH * (i + 1)] = own(b, me) + arrived(b, 2) + arrived(b, 5)
+        way = long_way(b)
+        long, short = slots(b)
+        if steps_of(b) == 4:
+            send_ring(b, long + 1, way, arrived(b, long) + own(b, 2 * way))
+        else:
+            send_ring(b, long + 2, way, arrived(b, long + 1) + own(b, way))
+        send_ring(b, short + 2, -way, arrived(b, short + 1) + own(b, -way))
+    hear(2)
+    for b in range(BLOCKS // 2):
+        way = long_way(b)
+        long, _ = slots(b)
+        send_ring(b, long + 2, way, arrived(b, long + 1) + own(b, way))
+    for h in (1, 0):
+        for i in range(2):
+            b = 2 * h + i
+            total[h, :, WIDTH * i : WIDTH * (i + 1)] = own(b, 0) + arrived(b, 2) + arrived(b, 5)
         value = total[h]
         peak = jnp.maximum(jnp.max(jnp.abs(value), axis=0, keepdims=True), 1e-30)
         power = jnp.floor(jnp.log2(peak)) + 1.0
@@ -259,17 +344,19 @@
         at = lax.broadcasted_iota(I32, (OWN, 1), 0)
         return jnp.where(at == 0, ref[0], jnp.where(at == 1, ref[1], ref[2]))
 
+    for copy in input_copies:
+        copy.wait()
     first_old = (
-        (codes1[...].astype(F32) - 7.5) / 7.5 * jnp.minimum(as_column(rows1), cols1[...])
-    )
-    level = (codes2[...].astype(F32) + 1.0) / 16.0
-    second_old = level * level * jnp.minimum(as_column(rows2), cols2[...])
-    steps = jnp.full((1, 128), step[0].astype(F32))
+        (codes_v[0].astype(F32) - 7.5) / 7.5 * jnp.minimum(as_column(rows1_s), cols_v[0])
+    )
+    level = (codes_v[1].astype(F32) + 1.0) / 16.0
+    second_old = level * level * jnp.minimum(as_column(rows2_s), cols_v[1])
+    steps = jnp.full((1, 128), step_s[0].astype(F32))
     first_fix = (1.0 - jnp.exp(steps * np.float32(np.log(0.9))))[:, 0:1]
     second_fix = (1.0 - jnp.exp(steps * np.float32(np.log(0.95))))[:, 0:1]
 
     parts = {}
-    for h in range(2):
+    for h in (1, 0):
         bytes_of(piece_in.at[h, pl.ds(0, PLANE - 1)], plane_recv.at[h])
         parts[h] = jnp.zeros((OWN, HALF), F32)
         for k in range(PLANE):
@@ -304,21 +391,33 @@
     first_new = 0.9 * first_old + 0.1 * clipped
     second_new = 0.95 * second_old + 0.05 * clipped * clipped
     ratio = first_new / first_fix / (jnp.sqrt(second_new / second_fix) + 1e-08)
-    new_master = master[...] - 0.001 * (ratio + 0.1 * master[...])
-    out_ratio[...] = ratio
-    out_master[...] = new_master
+    new_master = master_v[...] - 0.001 * (ratio + 0.1 * master_v[...])
 
     rounded = new_master.astype(BF16)
-    for h in range(2):
-        fresh[h] = rounded[:, h * HALF : (h + 1) * HALF]
-        near[h, place] = rounded[:, h * HALF : (h + 1) * HALF]
-
-        def send_near(k, h=h):
-            remote(
-                fresh.at[h], near.at[h, place], near_send.at[h], near_recv.at[h], in_plane(k)
-            ).start()
-
-        each_other(PLANE, place, send_near)
+    fresh[...] = rounded
+    near[place] = rounded
+    each_other(
+        PLANE,
+        place,
+        lambda k: remote(fresh, near.at[place], near_send, near_recv, in_plane(k)).start(),
+    )
+
+    results = (
+        (result_v.at[0], out_master),
+        (result_v.at[1], out_ratio),
+        (result_v.at[2], out_scaled1),
+        (result_v.at[3], out_scaled2),
+        (row_result, out_rows),
+        (col_result.at[0], out_cols1),
+        (col_result.at[1], out_cols2),
+    )
+    result_copies = [
+        pltpu.make_async_copy(src, dst, result_sem.at[i]) for i, (src, dst) in enumerate(results)
+    ]
+    result_v[0] = new_master
+    result_v[1] = ratio
+    result_copies[0].start()
+    result_copies[1].start()
 
     first_abs = jnp.abs(first_new)
     row_out[0] = jnp.broadcast_to(jnp.max(first_abs, axis=1, keepdims=True), (OWN, 128))
@@ -362,15 +461,13 @@
         copy.start()
         whole_copies[b, slot] = copy
 
-    for h in range(2):
-        bytes_of(near.at[h, pl.ds(0, PLANE - 1)], near_recv.at[h])
+    bytes_of(near.at[pl.ds(0, PLANE - 1)], near_recv)
+    for b in range(BLOCKS):
         for k in range(PLANE):
-            join[h, OWN * k : OWN * k + OWN] = near[h, k].astype(F32)
-        for i in range(4):
-            b = 4 * h + i
-            whole[b, me] = join[h, :, WIDTH * i : WIDTH * (i + 1)].astype(BF16)
-            pass_on(b, 0, 1, me)
-            pass_on(b, 3, -1, me)
+            join[b, OWN * k : OWN * k + OWN] = near[k, :, WIDTH * b : WIDTH * (b + 1)].astype(F32)
+        whole[b, me] = join[b].astype(BF16)
+        pass_on(b, 0, 1, me)
+        pass_on(b, 3, -1, me)
 
     bytes_of(col_in.at[0, pl.ds(0, PLANE - 1)], col_recv.at[0])
     best = jnp.max(col_in[0], axis=0)
@@ -389,7 +486,7 @@
             way = long_way(b)
             for first, direction in ((0, 1), (3, -1)):
                 whole_copies[b, first + s - 1].wait_recv()
-                if s == 2 and direction == way:
+                if s == 2 and direction == way and steps_of(b) == 3:
                     pass_on(b, 6, 2 * way, me - 2 * way)
                 pass_on(b, first + s, direction, me - direction * s)
 
@@ -409,22 +506,37 @@
     )
     bytes_of(row_in.at[pl.ds(0, 3)], row_recv)
     row_top = jnp.max(row_in[...], axis=0)
-    out_rows[...] = row_top
-
+    row_result[...] = row_top
+    result_copies[4].start()
+
+    for b in range(BLOCKS // 2):
+        way = long_way(b)
+        long, _ = slots(b)
+        whole_copies[b, long + 2].wait_recv()
+        pass_on(b, 6, way, me - 3 * way)
+
+    back_copy.wait()
     out_copies = []
-    for b in range(BLOCKS):
+    for b in (2, 3, 0, 1):
         for slot in (2, 5, 6):
-            whole_copies[b, slot].wait_recv()
-        copy = pltpu.make_async_copy(whole.at[b], out_whole.at[b], out_sem.at[b])
+            if steps_of(b) == 3 or slot != slots(b)[0] + 2:
+                whole_copies[b, slot].wait_recv()
+        block = whole[b].reshape(ROWS, WIDTH)
+        natural[b] = jnp.dot(back_v[...], block, preferred_element_type=F32).astype(BF16)
+        copy = pltpu.make_async_copy(
+            natural.at[b], out_natural.at[:, pl.ds(b * WIDTH, WIDTH)], out_sem.at[b]
+        )
         copy.start()
         out_copies.append(copy)
 
     bytes_of(col_in.at[2, pl.ds(0, PLANE - 1)], col_recv.at[2])
     for k in range(PLANE):
-        out_cols1[:, 128 * k : 128 * k + 128] = col_in[2, k, 0:1]
-        out_cols2[:, 128 * k : 128 * k + 128] = col_in[2, k, 1:2]
-    out_scaled1[...] = first_new / (jnp.minimum(row_top[0, :, 0:1], out_cols1[...]) + 1e-08)
-    out_scaled2[...] = second_new / (jnp.minimum(row_top[1, :, 0:1], out_cols2[...]) + 1e-08)
+        col_result[0, :, 128 * k : 128 * k + 128] = col_in[2, k, 0:1]
+        col_result[1, :, 128 * k : 128 * k + 128] = col_in[2, k, 1:2]
+    result_v[2] = first_new / (jnp.minimum(row_top[0, :, 0:1], col_result[0]) + 1e-08)
+    result_v[3] = second_new / (jnp.minimum(row_top[1, :, 0:1], col_result[1]) + 1e-08)
+    for i in (2, 3, 5, 6):
+        result_copies[i].start()
 
     for b in range(BLOCKS):
         bytes_of(ship.at[b], ring_send.at[b])
@@ -432,20 +544,20 @@
         bytes_of(whole.at[b, pl.ds(0, 7)], whole_send.at[b])
     for h in range(2):
         bytes_of(piece_out.at[h, pl.ds(0, PLANE - 1)], plane_send.at[h])
-        bytes_of(near.at[h, pl.ds(0, PLANE - 1)], near_send.at[h])
     for phase in range(2):
         bytes_of(norm_in.at[phase, pl.ds(0, 31 if phase else 15)], norm_send.at[phase])
     for phase in range(3):
         bytes_of(
             col_in.at[phase, pl.ds(0, 7 if phase == 1 else PLANE - 1)], col_send.at[phase]
         )
+    bytes_of(near.at[pl.ds(0, PLANE - 1)], near_send)
     bytes_of(row_in.at[pl.ds(0, 3)], row_send)
-    for copy in out_copies:
+    for copy in (*out_copies, *result_copies):
         copy.wait()
 
 
 def finish(
-    whole,
+    natural,
     master,
     ratio,
     scaled1,
@@ -453,7 +565,6 @@
     rows,
     cols1,
     cols2,
-    back,
     out_master,
     out_ratio,
     out_params,
@@ -463,61 +574,44 @@
     out_cols1,
     out_rows2,
     out_cols2,
-    whole_v,
-    back_v,
-    natural,
+    natural_v,
     own_v,
     col_v,
     row_v,
-    in_sem,
-    out_sem,
-    own_sem,
+    row1_s,
+    row2_s,
+    big_sem,
+    small_sem,
 ):
-    back_load = pltpu.make_async_copy(
-        back.at[lax.axis_index("mp_1")], back_v, own_sem.at[7]
-    )
-    back_load.start()
-    loads = [
-        pltpu.make_async_copy(whole.at[b], whole_v.at[b], in_sem.at[b]) for b in range(BLOCKS)
-    ]
-    for copy in loads:
-        copy.start()
+    moves = []
+    for i in range(RING):
+        at = pl.ds(i * CHUNK, CHUNK)
+        moves.append((natural.at[at], natural_v.at[at], out_params.at[at], big_sem.at[i]))
     sources = (master, ratio, scaled1, scaled2)
     targets = (out_master, out_ratio, out_scaled1, out_scaled2)
-    row_load = pltpu.make_async_copy(rows, row_v, own_sem.at[6])
+    for i in range(4):
+        moves.append((sources[i], own_v.at[i], targets[i], small_sem.at[i]))
+    moves.append((cols1, col_v.at[0], out_cols1, small_sem.at[4]))
+    moves.append((cols2, col_v.at[1], out_cols2, small_sem.at[5]))
+    row_load = pltpu.make_async_copy(rows, row_v, small_sem.at[6])
     row_load.start()
-    small = []
-    for i in range(4):
-        small.append((sources[i], own_v.at[i], targets[i], i))
-    small.append((cols1, col_v.at[0], out_cols1, 4))
-    small.append((cols2, col_v.at[1], out_cols2, 5))
-    ins = [pltpu.make_async_copy(src, at, own_sem.at[i]) for src, at, _, i in small]
+    ins = [pltpu.make_async_copy(src, at, sem) for src, at, _, sem in moves]
     for copy in ins:
         copy.start()
     outs = []
-    back_load.wait()
-    for q in range(PARTS):
-        loads[2 * q].wait()
-        loads[2 * q + 1].wait()
-        part = jnp.concatenate(
-            [whole_v[2 * q].reshape(ROWS, WIDTH), whole_v[2 * q + 1].reshape(ROWS, WIDTH)], axis=1
-        )
-        natural[q] = jnp.dot(back_v[...], part, preferred_element_type=F32).astype(BF16)
-        copy = pltpu.make_async_copy(
-            natural.at[q], out_params.at[:, pl.ds(q * PART, PART)], out_sem.at[q]
-        )
+    for load, (_, at, target, sem) in zip(ins, moves, strict=True):
+        load.wait()
+        copy = pltpu.make_async_copy(at, target, sem)
         copy.start()
         outs.append(copy)
-        if q == 0:
-            row_load.wait()
-            for j in range(OWN):
-                out_rows1[j] = jnp.max(row_v[0, j : j + 1])
-                out_rows2[j] = jnp.max(row_v[1, j : j + 1])
-            for load, (_, at, target, i) in zip(ins, small, strict=True):
-                load.wait()
-                copy = pltpu.make_async_copy(at, target, own_sem.at[i])
-                copy.start()
-                outs.append(copy)
+    row_load.wait()
+    for j in range(OWN):
+        row1_s[j] = jnp.max(row_v[0, j : j + 1])
+        row2_s[j] = jnp.max(row_v[1, j : j + 1])
+    for i, (src, dst) in enumerate(((row1_s, out_rows1), (row2_s, out_rows2))):
+        copy = pltpu.make_async_copy(src, dst, small_sem.at[6 + i])
+        copy.start()
+        outs.append(copy)
     for copy in outs:
         copy.wait()
 
@@ -551,27 +645,35 @@
     col = jax.ShapeDtypeStruct((1, COLS), F32)
     anywhere = pl.BlockSpec(memory_space=pl.ANY)
     hbm = pl.BlockSpec(memory_space=pltpu.HBM)
-    vmem = pl.BlockSpec(memory_space=pltpu.VMEM)
-    smem = pl.BlockSpec(memory_space=pltpu.SMEM)
     dma = pltpu.SemaphoreType.DMA
     perm, back = (jnp.asarray(p, BF16) for p in permutations())
-    new_master, ratio, whole, scaled1, scaled2, rows, cols1, cols2 = pl.pallas_call(
+    new_master, ratio, natural, scaled1, scaled2, rows, cols1, cols2 = pl.pallas_call(
         kernel,
         out_shape=(
             own,
             own,
-            jax.ShapeDtypeStruct((BLOCKS, RING, CHUNK, WIDTH), BF16),
+            jax.ShapeDtypeStruct((ROWS, COLS), BF16),
             own,
             own,
             jax.ShapeDtypeStruct((2, OWN, 128), F32),
             col,
             col,
         ),
-        in_specs=[hbm, hbm, vmem, vmem, vmem, smem, vmem, smem, vmem, smem, hbm],
-        out_specs=(vmem, vmem, anywhere, vmem, vmem, vmem, vmem, vmem),
+        in_specs=[hbm] * 12,
+        out_specs=(hbm,) * 8,
         scratch_shapes=[
+            pltpu.VMEM((OWN, COLS), F32),
+            pltpu.VMEM((2, OWN, COLS), I32),
+            pltpu.VMEM((2, 1, COLS), F32),
+            pltpu.SMEM((OWN,), F32),
+            pltpu.SMEM((OWN,), F32),
+            pltpu.SMEM((1,), I32),
+            pltpu.VMEM((4, OWN, COLS), F32),
+            pltpu.VMEM((2, OWN, 128), F32),
+            pltpu.VMEM((2, 1, COLS), F32),
             pltpu.VMEM((TOKENS, ROWS), BF16),
-            pltpu.VMEM((PARTS, TOKENS, PART), BF16),
+            pltpu.VMEM((BLOCKS, TOKENS, WIDTH), BF16),
+            pltpu.VMEM((ROWS, ROWS), BF16),
             pltpu.VMEM((ROWS, ROWS), BF16),
             pltpu.VMEM((ROWS, TOKENS), BF16),
             pltpu.VMEM((BLOCKS, RING, CHUNK, WIDTH), F32),
@@ -584,15 +686,20 @@
             pltpu.VMEM((2, PLANE, OWN + 1, HALF), I16),
             pltpu.VMEM((2, 1, 128), F32),
             pltpu.VMEM((2, 32, 1, 128), F32),
-            pltpu.VMEM((2, OWN, HALF), BF16),
-            pltpu.VMEM((2, PLANE, OWN, HALF), BF16),
-            pltpu.VMEM((2, CHUNK, HALF), F32),
+            pltpu.VMEM((OWN, COLS), BF16),
+            pltpu.VMEM((PLANE, OWN, COLS), BF16),
+            pltpu.VMEM((BLOCKS, CHUNK, WIDTH), F32),
             pltpu.VMEM((BLOCKS, RING, CHUNK, WIDTH), BF16),
+            pltpu.VMEM((BLOCKS, ROWS, WIDTH), BF16),
             pltpu.VMEM((3, PLANE, 2, 128), F32),
             pltpu.VMEM((3, PLANE, 2, 128), F32),
             pltpu.VMEM((2, OWN, 128), F32),
             pltpu.VMEM((4, 2, OWN, 128), F32),
-            dma((PARTS + 2,)),
+            pltpu.SemaphoreType.REGULAR((3,)),
+            dma((8,)),
+            dma((7,)),
+            dma((BLOCKS + 2,)),
+            dma,
             dma((BLOCKS,)),
             dma((BLOCKS,)),
             dma((BLOCKS, 7)),
@@ -600,10 +707,10 @@
             dma((BLOCKS, 7)),
             dma((2,)),
             dma((2,)),
-            dma((3,)),
-            dma((3,)),
             dma((2,)),
             dma((2,)),
+            dma,
+            dma,
             dma((BLOCKS,)),
             dma((BLOCKS, 7)),
             dma((3,)),
@@ -626,6 +733,7 @@
         second_cols.reshape(1, -1),
         step_count.reshape(1),
         perm,
+        back,
     )
     outs = pl.pallas_call(
         finish,
@@ -640,21 +748,20 @@
             row,
             col,
         ),
-        in_specs=[anywhere] * 8 + [hbm],
-        out_specs=(hbm, hbm, hbm, hbm, hbm, smem, hbm, smem, hbm),
+        in_specs=[anywhere] * 8,
+        out_specs=(hbm,) * 9,
         scratch_shapes=[
-            pltpu.VMEM((BLOCKS, RING, CHUNK, WIDTH), BF16),
-            pltpu.VMEM((ROWS, ROWS), BF16),
-            pltpu.VMEM((PARTS, ROWS, PART), BF16),
+            pltpu.VMEM((ROWS, COLS), BF16),
             pltpu.VMEM((4, OWN, COLS), F32),
             pltpu.VMEM((2, 1, COLS), F32),
             pltpu.VMEM((2, OWN, 128), F32),
-            dma((BLOCKS,)),
-            dma((BLOCKS,)),
+            pltpu.SMEM((OWN,), F32),
+            pltpu.SMEM((OWN,), F32),
+            dma((RING,)),
             dma((8,)),
         ],
         compiler_params=pltpu.CompilerParams(vmem_limit_bytes=60 * 1024 * 1024),
-    )(whole, new_master, ratio, scaled1, scaled2, rows, cols1, cols2, back)
+    )(natural, new_master, ratio, scaled1, scaled2, rows, cols1, cols2)
     outs = list(outs)
     outs[6] = outs[6].reshape(-1)
     outs[8] = outs[8].reshape(-1)

time: 79.2 us -> 74.7 us (0.943); the launches traced: 78.8 us -> 73.5 us
  Pallas kernels: 77.5 us -> 72.2 us
    pallas_call x1, Pallas kernels: 73.2 us -> 69.8 us  [shards(): pl.pallas_call(kernel, out_shape=(own, own, jax.ShapeDtypeStruct((ROWS, C...]
    pallas_call x1, Pallas kernels: 4.28 us -> 2.4 us  [shards(): pl.pallas_call(finish, out_shape=(own, own, jax.ShapeDtypeStruct((ROWS, C...]
where the time goes in v3:
time: 74.7 us; the launch traced here: 73.5 us
  Pallas kernels  72.2 us (97%)
  between operations  1.3 us (2%)
    pallas_call x1, Pallas kernels, shards(): pl.pallas_call(kernel, out_shape=(own, own, jax.ShapeDtypeStruct((ROWS, C...  69.8 us
    pallas_call x1, Pallas kernels, shards(): pl.pallas_call(finish, out_shape=(own, own, jax.ShapeDtypeStruct((ROWS, C...  2.4 us

profile of v3, /device:TPU:6, one launch (start us, length us, event | category | flops | bytes accessed | tf_op | source)
XLA Modules:
  0.0 73.5 jit_solution(14408231041704599213)
XLA Ops:
  1.3 69.8 %shard_map.187 = (f32[3,2048]{1,0:T(4,128)}, f32[3,2048]{1,0:T(4,128)}, bf16[384,2048]{1,0:T(8,128)(2,1)}, f32[3,2048]{1,0:T(4,128)}, f32[3,2048]{1,0:T(4,128)},...) custom-call(bf16[1024,384]{1,0:T(8,128)(2,1)} %hid.1, bf16[1024,2048]{1,0:T(8,128)(2,1)} %cot.1, ...), custom_call_target="tpu_custom_call" | custom-call | tf_op jit(solution)/shard_map/pallas_call | solution.py:650
  71.1 2.4 %shard_map.188 = (f32[3,2048]{1,0:T(4,128)}, f32[3,2048]{1,0:T(4,128)}, bf16[384,2048]{1,0:T(8,128)(2,1)}, f32[3,2048]{1,0:T(4,128)}, f32[3,2048]{1,0:T(4,128)},...) custom-call(bf16[384,2048]{1,0:T(8,128)(2,1)} %get-tuple-element.26.natural, ...), custom_call_target="tpu_custom_call" | custom-call | tf_op jit(solution)/shard_map/pallas_call | solution.py:738

commit v4 on v3

--- a/solution.py
+++ b/solution.py
@@ -91,10 +91,8 @@
     row_in,
     news,
     input_sem,
-    result_sem,
     local_sem,
     perm_sem,
-    out_sem,
     ring_send,
     ring_recv,
     scale_send,
@@ -106,7 +104,6 @@
     near_send,
     near_recv,
     whole_send,
-    whole_recv,
     col_send,
     col_recv,
     row_send,
@@ -117,15 +114,15 @@
     y = lax.axis_index("dp_2")
     xh = lax.axis_index("mp_0")
     core = lax.axis_index("mp_1")
-    me = y + core * (z - y)
-    other = z + core * (y - z)
+    me = z + core * (y - z)
+    other = y + core * (z - y)
     place = xl * 8 + other
     column = core * 8 + y
     sheet = (xl * 2 + xh) * 8 + z
     quad = xh * 2 + core
 
     def at(ring, across):
-        return {"dp_1": across + core * (ring - across), "dp_2": ring + core * (across - ring)}
+        return {"dp_1": ring + core * (across - ring), "dp_2": across + core * (ring - across)}
 
     def on_ring(c):
         return at(lax.rem(c + 16, 8), other)
@@ -225,12 +222,12 @@
         ship[b, slot] = coded.astype(I32).astype(I16)
         where = on_ring(me + distance)
         data = remote(
-            ship.at[b, slot], land.at[b, slot], ring_send.at[b], ring_recv.at[b, slot], where
+            ship.at[b, slot], land.at[b, slot], ring_send, ring_recv.at[b, slot], where
         )
         scale = remote(
             ship_scale.at[b, slot],
             land_scale.at[b, slot],
-            scale_send.at[b],
+            scale_send,
             scale_recv.at[b, slot],
             where,
         )
@@ -312,7 +309,9 @@
             send_ring(b, long + 2, way, arrived(b, long + 1) + own(b, way))
         send_ring(b, short + 2, -way, arrived(b, short + 1) + own(b, -way))
     hear(2)
-    for b in range(BLOCKS // 2):
+    for b in range(BLOCKS):
+        if steps_of(b) == 3:
+            continue
         way = long_way(b)
         long, _ = slots(b)
         send_ring(b, long + 2, way, arrived(b, long + 1) + own(b, way))
@@ -412,7 +411,7 @@
         (col_result.at[1], out_cols2),
     )
     result_copies = [
-        pltpu.make_async_copy(src, dst, result_sem.at[i]) for i, (src, dst) in enumerate(results)
+        pltpu.make_async_copy(src, dst, input_sem.at[i]) for i, (src, dst) in enumerate(results)
     ]
     result_v[0] = new_master
     result_v[1] = ratio
@@ -454,8 +453,8 @@
         copy = remote(
             whole.at[b, at],
             whole.at[b, at],
-            whole_send.at[b],
-            whole_recv.at[b, slot],
+            whole_send,
+            ring_recv.at[b, slot],
             on_ring(me + distance),
         )
         copy.start()
@@ -509,7 +508,9 @@
     row_result[...] = row_top
     result_copies[4].start()
 
-    for b in range(BLOCKS // 2):
+    for b in range(BLOCKS):
+        if steps_of(b) == 3:
+            continue
         way = long_way(b)
         long, _ = slots(b)
         whole_copies[b, long + 2].wait_recv()
@@ -524,7 +525,7 @@
         block = whole[b].reshape(ROWS, WIDTH)
         natural[b] = jnp.dot(back_v[...], block, preferred_element_type=F32).astype(BF16)
         copy = pltpu.make_async_copy(
-            natural.at[b], out_natural.at[:, pl.ds(b * WIDTH, WIDTH)], out_sem.at[b]
+            natural.at[b], out_natural.at[:, pl.ds(b * WIDTH, WIDTH)], local_sem.at[b]
         )
         copy.start()
         out_copies.append(copy)
@@ -538,10 +539,9 @@
     for i in (2, 3, 5, 6):
         result_copies[i].start()
 
-    for b in range(BLOCKS):
-        bytes_of(ship.at[b], ring_send.at[b])
-        bytes_of(ship_scale.at[b], scale_send.at[b])
-        bytes_of(whole.at[b, pl.ds(0, 7)], whole_send.at[b])
+    bytes_of(ship, ring_send)
+    bytes_of(ship_scale, scale_send)
+    bytes_of(whole.at[:, pl.ds(0, 7)], whole_send)
     for h in range(2):
         bytes_of(piece_out.at[h, pl.ds(0, PLANE - 1)], plane_send.at[h])
     for phase in range(2):
@@ -624,7 +624,7 @@
     to_y[natural, by_y] = 1.0
     to_z = np.zeros((ROWS, ROWS), np.float32)
     to_z[natural, by_z] = 1.0
-    there = np.stack([to_y, to_z])
+    there = np.stack([to_z, to_y])
     return there, there.transpose(0, 2, 1)
 
 
@@ -697,13 +697,11 @@
             pltpu.VMEM((4, 2, OWN, 128), F32),
             pltpu.SemaphoreType.REGULAR((3,)),
             dma((8,)),
-            dma((7,)),
             dma((BLOCKS + 2,)),
             dma,
-            dma((BLOCKS,)),
-            dma((BLOCKS,)),
+            dma,
             dma((BLOCKS, 7)),
-            dma((BLOCKS,)),
+            dma,
             dma((BLOCKS, 7)),
             dma((2,)),
             dma((2,)),
@@ -711,8 +709,7 @@
             dma((2,)),
             dma,
             dma,
-            dma((BLOCKS,)),
-            dma((BLOCKS, 7)),
+            dma,
             dma((3,)),
             dma((3,)),
             dma,

time: 74.7 us -> 73.9 us (0.989); the launches traced: 73.5 us -> 73.8 us
  no operation moved by 1% of the time
where the time goes in v4:
time: 73.9 us; the launch traced here: 73.8 us
  Pallas kernels  72.5 us (98%)
  between operations  1.3 us (2%)
    pallas_call x1, Pallas kernels, shards(): pl.pallas_call(kernel, out_shape=(own, own, jax.ShapeDtypeStruct((ROWS, C...  70.1 us
    pallas_call x1, Pallas kernels, shards(): pl.pallas_call(finish, out_shape=(own, own, jax.ShapeDtypeStruct((ROWS, C...  2.4 us

profile of v4, /device:TPU:6, one launch (start us, length us, event | category | flops | bytes accessed | tf_op | source)
XLA Modules:
  0.0 73.8 jit_solution(7423532927763529180)
XLA Ops:
  1.3 70.1 %shard_map.187 = (f32[3,2048]{1,0:T(4,128)}, f32[3,2048]{1,0:T(4,128)}, bf16[384,2048]{1,0:T(8,128)(2,1)}, f32[3,2048]{1,0:T(4,128)}, f32[3,2048]{1,0:T(4,128)},...) custom-call(bf16[1024,384]{1,0:T(8,128)(2,1)} %hid.1, bf16[1024,2048]{1,0:T(8,128)(2,1)} %cot.1, ...), custom_call_target="tpu_custom_call" | custom-call | tf_op jit(solution)/shard_map/pallas_call | solution.py:650
  71.4 2.4 %shard_map.188 = (f32[3,2048]{1,0:T(4,128)}, f32[3,2048]{1,0:T(4,128)}, bf16[384,2048]{1,0:T(8,128)(2,1)}, f32[3,2048]{1,0:T(4,128)}, f32[3,2048]{1,0:T(4,128)},...) custom-call(bf16[384,2048]{1,0:T(8,128)(2,1)} %get-tuple-element.26.natural, ...), custom_call_target="tpu_custom_call" | custom-call | tf_op jit(solution)/shard_map/pallas_call | solution.py:735
